TPU v7x, 32 devices: a whole 2x2x4 slice. The times are simulated.
32 devices in a mesh: dp: 2 (over x), tp: 4 (over z), fsdp: 4 (over y, core).
Axes of the slice: x: 2, y: 2, z: 4, core: 2. Of those that a mesh axis runs over, the one named last changes fastest.
Arguments:
- x: bfloat16 [8, 2048, 2048], P(('dp', 'fsdp')), parts along dimension 0
- w_query: bfloat16 [2, 2048, 2048], P(None, 'fsdp', 'tp')
- w_key: bfloat16 [2, 2048, 2048], P(None, 'fsdp', 'tp')
- w_value: bfloat16 [2, 2048, 2048], P(None, 'fsdp', 'tp')
- w_out: bfloat16 [2, 2048, 2048], P(None, 'tp', 'fsdp')
- w_gate: bfloat16 [2, 2048, 5504], P(None, 'fsdp', 'tp')
- w_up: bfloat16 [2, 2048, 5504], P(None, 'fsdp', 'tp')
- w_down: bfloat16 [2, 5504, 2048], P(None, 'tp', 'fsdp')
- q_norm_w: float32 [2, 2048], P(None, 'tp')
- k_norm_w: float32 [2, 2048], P(None, 'tp')
- attn_norm_w: float32 [2, 2048], P(None, 'fsdp')
- ffn_norm_w: float32 [2, 2048], P(None, 'fsdp')
Outputs:
- output 1: bfloat16 [8, 2048, 2048], P(('dp', 'fsdp')), parts along dimension 0
- output 2: bfloat16 [2, 8, 2048, 16, 128], P(None, ('dp', 'fsdp'), None, 'tp'), parts along dimension 1
- output 3: bfloat16 [2, 8, 2048, 16, 128], P(None, ('dp', 'fsdp'), None, 'tp'), parts along dimension 1
There are 2 independent parts. A program takes and returns all parts, laid end to end along the dimension named above; an argument that names none is the same for every part.
All inputs are finite; a program needn't handle non-finite values.
Results may differ from a plain program's by a relative error of at most 0.02.
Values are sent between devices in bfloat16 or wider.
A program may use at most 1 GiB of HBM per device.

v0:
```python
import jax
import jax.numpy as jnp
from jax import lax
from jax.sharding import PartitionSpec as P

HEAD_DIM = 128
NORM_EPS = 1e-6
ROPE_THETA = 500000.0


def rope_tables(seq_len):
    half = HEAD_DIM // 2
    inv_freq = ROPE_THETA ** (-2.0 * jnp.arange(half, dtype=jnp.float32) / HEAD_DIM)
    angles = jnp.arange(seq_len, dtype=jnp.float32)[:, None] * inv_freq[None, :]
    return jnp.cos(angles)[:, None, :], jnp.sin(angles)[:, None, :]


def apply_rope(vals, cos_t, sin_t):
    half = HEAD_DIM // 2
    first = vals[..., :half]
    second = vals[..., half:]
    return jnp.concatenate([first * cos_t - second * sin_t, second * cos_t + first * sin_t], axis=-1)


def rms_scale(vals):
    return lax.rsqrt(jnp.mean(vals * vals, axis=-1, keepdims=True) + NORM_EPS)


def attend(queries, keys_rot, values, causal):
    scores = jnp.einsum('bqhd,bkhd->bhqk', queries, keys_rot, preferred_element_type=jnp.float32) * (HEAD_DIM ** -0.5)
    scores = jnp.where(causal, scores, -jnp.inf)
    attn_probs = jax.nn.softmax(scores, axis=-1).astype(jnp.bfloat16)
    return jnp.einsum('bhqk,bkhd->bqhd', attn_probs, values, preferred_element_type=jnp.float32).astype(jnp.bfloat16)


def solution(mesh):
    batch_axes = ('dp', 'fsdp')
    act_spec = P(batch_axes, None, None)
    in_cols = P(None, 'fsdp', 'tp')
    in_rows = P(None, 'tp', 'fsdp')
    tp_gain = P(None, 'tp')
    fsdp_gain = P(None, 'fsdp')
    cache_spec = P(None, batch_axes, None, 'tp', None)

    def local_layers(x, w_query, w_key, w_value, w_out, w_gate, w_up, w_down, q_norm_w, k_norm_w, attn_norm_w, ffn_norm_w):
        batch, seq_len, width = x.shape
        tokens = batch * seq_len
        head_shape = (batch, seq_len, w_query.shape[2] // HEAD_DIM, HEAD_DIM)
        cos_t, sin_t = rope_tables(seq_len)
        causal = jnp.arange(seq_len)[:, None] >= jnp.arange(seq_len)[None, :]
        hidden = x.reshape(tokens, width)
        k_layers = []
        v_layers = []
        for layer in range(w_query.shape[0]):
            wq_full = lax.all_gather(w_query[layer], 'fsdp', axis=0, tiled=True)
            wk_full = lax.all_gather(w_key[layer], 'fsdp', axis=0, tiled=True)
            wv_full = lax.all_gather(w_value[layer], 'fsdp', axis=0, tiled=True)
            q_raw = jnp.dot(hidden, wq_full, preferred_element_type=jnp.float32)
            k_raw = jnp.dot(hidden, wk_full, preferred_element_type=jnp.float32)
            values = jnp.dot(hidden, wv_full, preferred_element_type=jnp.float32).astype(jnp.bfloat16).reshape(head_shape)
            sq_local = jnp.stack([jnp.sum(q_raw * q_raw, axis=-1), jnp.sum(k_raw * k_raw, axis=-1)])
            sq_total = lax.psum(sq_local, 'tp')
            inv_rms = lax.rsqrt(sq_total / width + NORM_EPS)
            queries = apply_rope((q_raw * inv_rms[0][:, None] * q_norm_w[layer]).reshape(head_shape), cos_t, sin_t).astype(jnp.bfloat16)
            keys_rot = apply_rope((k_raw * inv_rms[1][:, None] * k_norm_w[layer]).reshape(head_shape), cos_t, sin_t).astype(jnp.bfloat16)
            attended = attend(queries, keys_rot, values, causal)
            wo_full = lax.all_gather(w_out[layer], 'fsdp', axis=1, tiled=True)
            a_part = jnp.dot(attended.reshape(tokens, -1), wo_full, preferred_element_type=jnp.float32).astype(jnp.bfloat16)
            a_out = lax.psum(a_part, 'tp').astype(jnp.float32)
            attn_gain = lax.all_gather(attn_norm_w[layer], 'fsdp', axis=0, tiled=True)
            h_new = (hidden.astype(jnp.float32) + a_out * rms_scale(a_out) * attn_gain).astype(jnp.bfloat16)
            wg_full = lax.all_gather(w_gate[layer], 'fsdp', axis=0, tiled=True)
            wu_full = lax.all_gather(w_up[layer], 'fsdp', axis=0, tiled=True)
            gate = jnp.dot(h_new, wg_full, preferred_element_type=jnp.float32)
            up_val = jnp.dot(h_new, wu_full, preferred_element_type=jnp.float32)
            hidden_act = (jax.nn.silu(gate) * up_val).astype(jnp.bfloat16)
            wd_full = lax.all_gather(w_down[layer], 'fsdp', axis=1, tiled=True)
            m_part = jnp.dot(hidden_act, wd_full, preferred_element_type=jnp.float32).astype(jnp.bfloat16)
            m_out = lax.psum(m_part, 'tp').astype(jnp.float32)
            ffn_gain = lax.all_gather(ffn_norm_w[layer], 'fsdp', axis=0, tiled=True)
            hidden = (h_new.astype(jnp.float32) + m_out * rms_scale(m_out) * ffn_gain).astype(jnp.bfloat16)
            k_layers.append(keys_rot)
            v_layers.append(values)
        return hidden.reshape(batch, seq_len, width), jnp.stack(k_layers), jnp.stack(v_layers)

    return jax.shard_map(local_layers, mesh=mesh,
                         in_specs=(act_spec, in_cols, in_cols, in_cols, in_rows, in_cols, in_cols, in_rows,
                                   tp_gain, tp_gain, fsdp_gain, fsdp_gain),
                         out_specs=(act_spec, cache_spec, cache_spec), check_vma=False)
```

profile of v0, /device:TPU:0, one launch (start us, length us, event | category | flops | bytes accessed | tf_op | source)
XLA Modules:
  0.0 1925.3 jit_solution(7122705763248801941)
XLA Ops:
  23.4 11.9 all-gather.35.cloned.1.call-done
  45.8 13.9 all-gather.37.cloned.1.call-done
  70.6 18.7 psum.42
  124.1 38.4 %fusion.115 = f32[4,2048]{1,0:T(4,128)S(1)} fusion(pred[2048,2048]{0,1:T(8,128)(4,1)} %iota_compare_fusion, bf16[2048,4,64]{2,0,1:T(8,128)(2,1)} %bitcast.134, bf16[2048,4,64]{2,0,1:T(8,128)(2,1)} %bitcast.137, bf16[2048,4,64]{2,0,1:T(8,128)(2,1)} %get-tuple-element.14, bf16[2048,4,64]{2,0,1:T(8,128)(2,1)} %get-tuple-element.13), kind=kOutput, calls=%fused_computation.147 | convolution fusion | flops 4370466816 | bytes 8421376 | tf_op jit(solution)/shard_map/sub | solution.py:32
  172.5 38.7 %fusion.65 = bf16[4,128,2048]{2,1,0:T(8,128)(2,1)} fusion(bf16[2048,4,128]{0,2,1:T(8,128)(2,1)} %bitcast.146, f32[4,2048]{1,0:T(4,128)S(1)} %fusion.115, pred[2048,2048]{0,1:T(8,128)(4,1)} %iota_compare_fusion, bf16[2048,4,64]{2,0,1:T(8,128)(2,1)S(1)} %bitcast.136, bf16[2048,4,64]{2,0,1:T(8,128)(2,1)} %bitcast.138, ...), kind=kOutput, calls=%fused_computation.89 | convolution fusion | flops 8683268096 | bytes 12615680 | tf_op jit(solution)/shard_map/bhqk,bkhd->bqhd/dot_general | solution.py:33
  236.5 271.1 %all-reduce.5.cloned.1.call-done = bf16[2048,2048]{1,0:T(8,128)(2,1)} async-done(((bf16[2048,2048]{1,0:T(8,128)(2,1)}), bf16[2048,2048]{1,0:T(8,128)(2,1)}) %all-reduce.5.cloned.1.call-update) | async-done | bytes 8388624 | tf_op jit(solution)/shard_map/psum | solution.py:69
  522.7 28.0 %all-gather.41.cloned.1.call-done = bf16[1,2048,1376]{1,2,0:T(8,128)(2,1)} async-done(((bf16[1,512,1376]{1,2,0:T(8,128)(2,1)}), bf16[1,2048,1376]{1,2,0:T(8,128)(2,1)}) %all-gather.41.cloned.1.call-update) | async-done | bytes 5636112 | tf_op jit(solution)/shard_map/all_gather | solution.py:72
  550.7 18.4 fusion.55
  569.1 25.8 %all-gather.43.cloned.1.call-done = bf16[1,2048,1376]{1,2,0:T(8,128)(2,1)} async-done(((bf16[1,512,1376]{1,2,0:T(8,128)(2,1)}), bf16[1,2048,1376]{1,2,0:T(8,128)(2,1)}) %all-gather.43.cloned.1.call-update) | async-done | bytes 5636112 | tf_op jit(solution)/shard_map/all_gather | solution.py:73
  594.9 44.8 %all-gather.45.cloned.1.call-done = bf16[1,1376,2048]{2,1,0:T(8,128)(2,1)} async-done(((bf16[1,1376,512]{2,1,0:T(8,128)(2,1)}), bf16[1,1376,2048]{2,1,0:T(8,128)(2,1)}) %all-gather.45.cloned.1.call-update) | async-done | bytes 5636112 | tf_op jit(solution)/shard_map/all_gather | solution.py:77
  639.7 36.0 %convolution_convert_fusion.2 = bf16[2048,2048]{1,0:T(8,128)(2,1)} fusion(bf16[1,1376,2048]{2,1,0:T(8,128)(2,1)} %all-gather.45.cloned.1.call-done, f32[2048,1376]{0,1:T(8,128)} %fusion.55, bf16[2048,2048]{1,0:T(8,128)(2,1)} %fusion.15, bf16[1,2048,1376]{1,2,0:T(8,128)(2,1)} %all-gather.43.cloned.1.call-done), kind=kOutput, calls=%fused_computation.56 | convolution fusion | flops 23106551808 | bytes 39321600 | tf_op jit(solution)/shard_map/dot_general | solution.py:78
  684.2 280.4 %all-reduce.7.cloned.1.call-done = bf16[2048,2048]{1,0:T(8,128)(2,1)} async-done(((bf16[2048,2048]{1,0:T(8,128)(2,1)}), bf16[2048,2048]{1,0:T(8,128)(2,1)}) %all-reduce.7.cloned.1.call-update) | async-done | bytes 8388624 | tf_op jit(solution)/shard_map/psum | solution.py:79
  997.9 13.3 all-gather.51.cloned.1.call-done
  1021.8 19.3 %psum.45 = f32[2,2048]{1,0:T(2,128)S(1)} all-reduce(f32[2,2048]{1,0:T(2,128)S(1)} %pad_maximum_fusion.6), channel_id=1, replica_groups=mesh['dp'=2,'tp'=4,'fsdp'=4] {'tp'}, use_global_device_ids=true, to_apply=%region_11.12 | all-reduce | flops 4096 | bytes 32768 | tf_op jit(solution)/shard_map/psum | solution.py:62
  1072.8 29.0 %fusion.116 = f32[4,2048]{1,0:T(4,128)S(1)} fusion(pred[2048,2048]{0,1:T(8,128)(4,1)} %iota_compare_fusion, bf16[2048,4,64]{2,0,1:T(8,128)(2,1)} %bitcast.140, bf16[2048,4,64]{2,0,1:T(8,128)(2,1)} %bitcast.143, bf16[2048,4,64]{2,0,1:T(8,128)(2,1)} %get-tuple-element.10, bf16[2048,4,64]{2,0,1:T(8,128)(2,1)} %get-tuple-element.9), kind=kOutput, calls=%fused_computation.148 | convolution fusion | flops 4370466816 | bytes 8421376 | tf_op jit(solution)/shard_map/sub | solution.py:32
  1111.9 38.7 %fusion.62 = bf16[4,128,2048]{2,1,0:T(8,128)(2,1)} fusion(bf16[2048,4,128]{0,2,1:T(8,128)(2,1)} %bitcast.148, f32[4,2048]{1,0:T(4,128)S(1)} %fusion.116, pred[2048,2048]{0,1:T(8,128)(4,1)} %iota_compare_fusion, bf16[2048,4,64]{2,0,1:T(8,128)(2,1)S(1)} %bitcast.142, bf16[2048,4,64]{2,0,1:T(8,128)(2,1)} %bitcast.144, ...), kind=kOutput, calls=%fused_computation.88 | convolution fusion | flops 8683268096 | bytes 12615680 | tf_op jit(solution)/shard_map/bhqk,bkhd->bqhd/dot_general | solution.py:33
  1167.8 279.2 %all-reduce.9.cloned.1.call-done = bf16[2048,2048]{1,0:T(8,128)(2,1)} async-done(((bf16[2048,2048]{1,0:T(8,128)(2,1)}), bf16[2048,2048]{1,0:T(8,128)(2,1)}) %all-reduce.9.cloned.1.call-update) | async-done | bytes 8388624 | tf_op jit(solution)/shard_map/psum | solution.py:69
  1462.0 27.9 %all-gather.55.cloned.1.call-done = bf16[1,2048,1376]{1,2,0:T(8,128)(2,1)} async-done(((bf16[1,512,1376]{1,2,0:T(8,128)(2,1)}), bf16[1,2048,1376]{1,2,0:T(8,128)(2,1)}) %all-gather.55.cloned.1.call-update) | async-done | bytes 5636112 | tf_op jit(solution)/shard_map/all_gather | solution.py:72
  1490.0 18.4 fusion.50
  1508.4 25.6 %all-gather.57.cloned.1.call-done = bf16[1,2048,1376]{1,2,0:T(8,128)(2,1)} async-done(((bf16[1,512,1376]{1,2,0:T(8,128)(2,1)}), bf16[1,2048,1376]{1,2,0:T(8,128)(2,1)}) %all-gather.57.cloned.1.call-update) | async-done | bytes 5636112 | tf_op jit(solution)/shard_map/all_gather | solution.py:73
  1534.0 44.0 %all-gather.59.cloned.1.call-done = bf16[1,1376,2048]{2,1,0:T(8,128)(2,1)} async-done(((bf16[1,1376,512]{2,1,0:T(8,128)(2,1)}), bf16[1,1376,2048]{2,1,0:T(8,128)(2,1)}) %all-gather.59.cloned.1.call-update) | async-done | bytes 5636112 | tf_op jit(solution)/shard_map/all_gather | solution.py:77
  1578.1 36.0 %convolution_convert_fusion = bf16[2048,2048]{1,0:T(8,128)(2,1)} fusion(bf16[1,1376,2048]{2,1,0:T(8,128)(2,1)} %all-gather.59.cloned.1.call-done, f32[2048,1376]{0,1:T(8,128)} %fusion.50, bf16[2048,2048]{1,0:T(8,128)(2,1)} %fusion.23, bf16[1,2048,1376]{1,2,0:T(8,128)(2,1)} %all-gather.57.cloned.1.call-done), kind=kOutput, calls=%fused_computation.54 | convolution fusion | flops 23106551808 | bytes 39321600 | tf_op jit(solution)/shard_map/dot_general | solution.py:78
  1627.9 20.5 %copy.36 = bf16[2,1,2048,4,128]{4,3,2,1,0:T(4,128)(2,1)} copy(bf16[2,1,2048,4,128]{4,2,3,1,0:T(8,128)(2,1)S(1)} %maximum_maximum_fusion) | data formatting | bytes 8388608
  1658.5 244.5 %all-reduce.11.cloned.1.call-done = bf16[2048,2048]{1,0:T(8,128)(2,1)} async-done(((bf16[2048,2048]{1,0:T(8,128)(2,1)}), bf16[2048,2048]{1,0:T(8,128)(2,1)}) %all-reduce.11.cloned.1.call-update) | async-done | bytes 8388624 | tf_op jit(solution)/shard_map/psum | solution.py:79
  (151 shorter events, 287.7 us)
Async XLA Ops:
  7.2 6.0 copy-start.13
  7.2 28.1 %all-gather.35.cloned.1.call-start = ((), (), s32[]{:S(2)}) async-start(), calls=%async_computation.5 | async-start | bytes 2621440 | tf_op jit(solution)/shard_map/all_gather | solution.py:55
  9.6 50.1 %all-gather.37.cloned.1.call-start = ((), (), s32[]{:S(2)}) async-start(), calls=%async_computation.6 | async-start | bytes 2621440 | tf_op jit(solution)/shard_map/all_gather | solution.py:56
  11.9 150.6 %all-gather.33.cloned.1.call-start = ((), (), s32[]{:S(2)}) async-start(), calls=%async_computation.4 | async-start | bytes 2621440 | tf_op jit(solution)/shard_map/all_gather | solution.py:57
  13.1 198.2 %all-gather.39.cloned.1.call-start = ((), (), s32[]{:S(2)}) async-start(), calls=%async_computation.7 | async-start | bytes 2621440 | tf_op jit(solution)/shard_map/all_gather | solution.py:67
  14.2 493.5 %all-reduce.5.cloned.1.call-start = ((), (), s32[]{:S(2)}) async-start(), calls=%async_computation | async-start | bytes 16777216 | tf_op jit(solution)/shard_map/psum | solution.py:69
  23.3 91.2 %copy-start.4 = (f32[2048,64]{1,0:T(8,128)}, f32[2048,64]{1,0:T(8,128)S(1)}, u32[]{:S(2)}) copy-start(f32[2048,64]{1,0:T(8,128)S(1)} %get-tuple-element.55) | copy-start | bytes 1572868
  23.4 91.2 %copy-start.6 = (f32[2048,64]{1,0:T(8,128)}, f32[2048,64]{1,0:T(8,128)S(1)}, u32[]{:S(2)}) copy-start(f32[2048,64]{1,0:T(8,128)S(1)} %get-tuple-element.56) | copy-start | bytes 1572868
  162.5 10.1 copy-start.8
  221.5 329.2 %all-gather.41.cloned.1.call-start = ((), (), s32[]{:S(2)}) async-start(), calls=%async_computation.8 | async-start | bytes 7045120 | tf_op jit(solution)/shard_map/all_gather | solution.py:72
  225.1 369.8 %all-gather.43.cloned.1.call-start = ((), (), s32[]{:S(2)}) async-start(), calls=%async_computation.9 | async-start | bytes 7045120 | tf_op jit(solution)/shard_map/all_gather | solution.py:73
  228.9 410.8 %all-gather.45.cloned.1.call-start = ((), (), s32[]{:S(2)}) async-start(), calls=%async_computation.10 | async-start | bytes 7045120 | tf_op jit(solution)/shard_map/all_gather | solution.py:77
  230.7 733.9 %all-reduce.7.cloned.1.call-start = ((), (), s32[]{:S(2)}) async-start(), calls=%async_computation.1 | async-start | bytes 16777216 | tf_op jit(solution)/shard_map/psum | solution.py:79
  675.7 311.6 %all-gather.49.cloned.1.call-start = ((), (), s32[]{:S(2)}) async-start(), calls=%async_computation.12 | async-start | bytes 2621440 | tf_op jit(solution)/shard_map/all_gather | solution.py:55
  676.3 334.9 %all-gather.51.cloned.1.call-start = ((), (), s32[]{:S(2)}) async-start(), calls=%async_computation.13 | async-start | bytes 2621440 | tf_op jit(solution)/shard_map/all_gather | solution.py:56
  677.1 424.8 %all-gather.47.cloned.1.call-start = ((), (), s32[]{:S(2)}) async-start(), calls=%async_computation.11 | async-start | bytes 2621440 | tf_op jit(solution)/shard_map/all_gather | solution.py:57
  677.6 473.1 %all-gather.53.cloned.1.call-start = ((), (), s32[]{:S(2)}) async-start(), calls=%async_computation.14 | async-start | bytes 2621440 | tf_op jit(solution)/shard_map/all_gather | solution.py:67
  678.4 768.5 %all-reduce.9.cloned.1.call-start = ((), (), s32[]{:S(2)}) async-start(), calls=%async_computation.2 | async-start | bytes 16777216 | tf_op jit(solution)/shard_map/psum | solution.py:69
  997.9 43.2 %copy-start.17 = (f32[1,512]{1,0:T(1,128)S(1)}, f32[1,512]{1,0:T(1,128)}, u32[]{:S(2)}) copy-start(f32[1,512]{1,0:T(1,128)} %get-tuple-element.53) | copy-start | bytes 6148
  1101.9 10.0 copy-start.9
  1160.8 329.2 %all-gather.55.cloned.1.call-start = ((), (), s32[]{:S(2)}) async-start(), calls=%async_computation.15 | async-start | bytes 7045120 | tf_op jit(solution)/shard_map/all_gather | solution.py:72
  1161.4 372.6 %all-gather.57.cloned.1.call-start = ((), (), s32[]{:S(2)}) async-start(), calls=%async_computation.16 | async-start | bytes 7045120 | tf_op jit(solution)/shard_map/all_gather | solution.py:73
  1162.0 416.1 %all-gather.59.cloned.1.call-start = ((), (), s32[]{:S(2)}) async-start(), calls=%async_computation.17 | async-start | bytes 7045120 | tf_op jit(solution)/shard_map/all_gather | solution.py:77
  1162.6 740.4 %all-reduce.11.cloned.1.call-start = ((), (), s32[]{:S(2)}) async-start(), calls=%async_computation.3 | async-start | bytes 16777216 | tf_op jit(solution)/shard_map/psum | solution.py:79
  (16 other events, 62.7 us)
Sparse Core Ops, SparseCore 0:
  10.1 25.0 all-gather.34
  37.4 22.3 all-gather.36
  61.3 22.3 all-gather.32
  85.1 22.3 all-gather.38
  221.7 285.9 all-reduce.4
  509.1 41.5 all-gather.40
  552.3 42.5 all-gather.42
  597.0 42.5 all-gather.44
  675.9 288.7 all-reduce.6
  966.0 21.2 all-gather.48
  988.9 22.3 all-gather.50
  1012.7 22.3 all-gather.46
  1036.6 22.3 all-gather.52
  1160.9 285.9 all-reduce.8
  1448.3 41.5 all-gather.54
  1491.4 42.5 all-gather.56
  1535.4 42.5 all-gather.58
  1614.2 288.7 all-reduce.10
where the time goes:
time: 1940 us; the launch traced here: 1930 us
  waiting for transfers between devices  1320 us (68%)
  matrix products  337 us (17%)
  other arithmetic  107 us (6%)
  local copies, waits for them, and re-layouts  85.4 us (4%)
  blocking collectives  58.6 us (3%)
    psum x2, waiting for transfers between devices, local_layers(): a_out = lax.psum(a_part, 'tp').astype(jnp.float32)  550 us
    psum x2, waiting for transfers between devices, local_layers(): m_out = lax.psum(m_part, 'tp').astype(jnp.float32)  525 us
    all_gather x2, waiting for transfers between devices, local_layers(): wd_full = lax.all_gather(w_down[layer], 'fsdp', axis=1, tiled=True)  88.8 us
    dot_general x2, matrix products, attend(): jnp.einsum('bhqk,bkhd->bqhd', attn_probs, values, preferred_element_type=...  77.5 us
    dot_general x2, matrix products, local_layers(): jnp.dot(hidden_act, wd_full, preferred_element_type=jnp.float32)  72 us
    sub x2, matrix products, attend(): attn_probs = jax.nn.softmax(scores, axis=-1).astype(jnp.bfloat16)  67.4 us
    all_gather x2, waiting for transfers between devices, local_layers(): wg_full = lax.all_gather(w_gate[layer], 'fsdp', axis=0, tiled=True)  55.9 us
    unnamed x53, local copies, waits for them, and re-layouts  53.7 us
  transfers between devices with their start and end apart: 18, of which 14 were waited for; matrix products, arithmetic and copies ran while one was open for 22% of the time, Pallas kernels for 0%

commit v1 on v0

v1 whole, which is shorter than its diff:
```python
import functools
import jax
import jax.numpy as jnp
import numpy as np
from jax import lax
from jax.experimental import pallas as pl
from jax.experimental.pallas import tpu as pltpu
from jax.sharding import PartitionSpec as P

HEAD_DIM = 128
NORM_EPS = 1e-6
ROPE_THETA = 500000.0
LOG2E = 1.4426950408889634
MESH = pl.DeviceIdType.MESH
BF16 = jnp.bfloat16
F32 = jnp.float32
N_SEM = 240
D_CUT = 352


def rope_table(seq_len):
    half = HEAD_DIM // 2
    inv_freq = np.float32(ROPE_THETA) ** (-2.0 * np.arange(half, dtype=np.float32) / np.float32(HEAD_DIM))
    angles = np.arange(seq_len, dtype=np.float32)[:, None] * inv_freq.astype(np.float32)[None, :]
    return np.concatenate([np.cos(angles), np.sin(angles)], axis=1).astype(np.float32)


def dot_nt(lhs, rhs):
    return lax.dot_general(lhs, rhs, (((1,), (1,)), ((), ())), preferred_element_type=F32)


def dot_nn(lhs, rhs):
    return jnp.dot(lhs, rhs, preferred_element_type=F32)


def loop(count, body):
    lax.fori_loop(0, count, lambda i, c: (body(i), c)[1], 0)


def mega(x_ref, wq_ref, wk_ref, wv_ref, wo_ref, wg_ref, wu_ref, wd_ref, gain_ref, tab_ref,
         y_ref, kc_ref, vc_ref, aq_ref, ao_ref, ag_ref, au_ref, ad_ref,
         xbuf, hb, ofull, sqb, cosb, sinb, gp, send_sems, recv_sems, loc_sems):
    seq = x_ref.shape[0]
    chunk = seq // 4
    cx, cz, cf = lax.axis_index('dp'), lax.axis_index('tp'), lax.axis_index('fsdp')
    f1 = cf + 1 - 2 * (cf % 2)
    f2 = (cf + 2) % 4
    nx = 1 - cx
    up_z = (cz + 1) % 4
    X = (nx, cz, cf)
    Y = (cx, cz, f2)
    C = (cx, cz, f1)
    Z = (cx, up_z, cf)
    state = {'n': 0}
    sent = []

    def remote(pairs, dev):
        out = []
        for src, dst in pairs:
            n = state['n']
            state['n'] = n + 1
            cp = pltpu.make_async_remote_copy(src_ref=src, dst_ref=dst, send_sem=send_sems.at[n], recv_sem=recv_sems.at[n],
                                              device_id=dev, device_id_type=MESH)
            cp.start()
            out.append((n, frozen(src), frozen(dst)))
        sent.extend(out)
        return out

    def frozen(ref):
        if not getattr(ref, 'transforms', ()):
            return ref, None
        idx, = ref.transforms
        return ref.ref, tuple(int(i.size) if isinstance(i, pl.Slice) else None for i in idx.indices)

    def thawed(item):
        ref, sizes = item
        return ref if sizes is None else ref.at[tuple(0 if s is None else pl.ds(0, s) for s in sizes)]

    def handle(n, src, dst):
        return pltpu.make_async_remote_copy(src_ref=thawed(src), dst_ref=thawed(dst), send_sem=send_sems.at[n], recv_sem=recv_sems.at[n],
                                            device_id=(0, 0, 0), device_id_type=MESH)

    def arrive(cps):
        for cp in cps:
            handle(*cp).wait_recv()

    def flush(cp):
        handle(*cp).wait_send()

    def rows(base, size):
        return pl.ds(base if isinstance(base, int) else pl.multiple_of(base, 16), size)

    class Group:
        def __init__(self, kind, layer):
            self.kind, self.layer, self.tx = kind, layer, {}

        def whole(self, p, f):
            l = self.layer
            if self.kind == 'q':
                return [aq_ref.at[l, i, rows(f * 512, 512), :] for i in range(3)]
            if self.kind == 'o':
                return [ao_ref.at[l, p, f]]
            return [ag_ref.at[l, p, rows(f * 512, 512), :], au_ref.at[l, p, rows(f * 512, 512), :], ad_ref.at[l, p, f]]

        def half(self, p, f, xh):
            l = self.layer
            if self.kind == 'q':
                return [aq_ref.at[l, i, rows(f * 512 + xh * 256, 256), :] for i in range(3)]
            if self.kind == 'o':
                return [ao_ref.at[l, p, f, rows(xh * 256, 256), :]]
            r = rows(f * 512 + xh * 256, 256)
            return [ag_ref.at[l, p, r, :], au_ref.at[l, p, r, :], ad_ref.at[l, p, f, rows(xh * 688, 688), :]]

        def via_x(self, p, f, xh):
            l = self.layer
            if self.kind == 'o':
                return [ao_ref.at[l, p, f, rows(xh * 256, 128), :]]
            return [ag_ref.at[l, p, rows(f * 512 + xh * 256, 256), :], ad_ref.at[l, p, f, rows(xh * 688, D_CUT), :]]

        def via_y(self, p, f, xh):
            l = self.layer
            if self.kind == 'o':
                return [ao_ref.at[l, p, f, rows(xh * 256 + 128, 128), :]]
            return [au_ref.at[l, p, rows(f * 512 + xh * 256, 256), :],
                    ad_ref.at[l, p, f, rows(xh * 688 + D_CUT, 688 - D_CUT), :]]

        def own_whole(self):
            l = self.layer
            if self.kind == 'q':
                return [r.at[l] for r in (wq_ref, wk_ref, wv_ref)]
            if self.kind == 'o':
                return [wo_ref.at[l]]
            return [wg_ref.at[l], wu_ref.at[l], wd_ref.at[l]]

        def own_half(self):
            l = self.layer
            if self.kind == 'q':
                return [r.at[l, rows(cx * 256, 256), :] for r in (wq_ref, wk_ref, wv_ref)]
            if self.kind == 'o':
                return [wo_ref.at[l, rows(cx * 256, 256), :]]
            return [wg_ref.at[l, rows(cx * 256, 256), :], wu_ref.at[l, rows(cx * 256, 256), :],
                    wd_ref.at[l, rows(cx * 688, 688), :]]

        def plane(self, k):
            return (cz + 4 - k) % 4

        def begin_plane(self):
            self.tx['y0'] = remote(zip(self.own_half(), self.half(cz, cf, cx)), Y)
            self.tx['c0'] = remote(zip(self.own_whole(), self.whole(cz, cf)), C)

        def begin_ring(self):
            self.tx['z1'] = remote(zip(self.own_half(), self.half(cz, cf, cx)), Z)

        def got_y0(self):
            arrive(self.tx['y0'])
            refs = self.half(cz, f2, cx)
            self.tx['rx0'] = remote(zip(refs, refs), X)

        def got_rx0(self):
            arrive(self.tx['rx0'])
            refs = self.whole(cz, f2)
            self.tx['d0'] = remote(zip(refs, refs), C)

        def got_z(self, k):
            arrive(self.tx[f'z{k}'])
            refs = self.half(self.plane(k), cf, cx)
            if k < 3:
                self.tx[f'z{k + 1}'] = remote(zip(refs, refs), Z)
            self.tx[f'x{k}'] = remote(zip(refs, refs), X)
            self.tx[f'y{k}'] = remote(zip(refs, refs), Y)

        def got_x(self, k):
            arrive(self.tx[f'x{k}'])
            p = self.plane(k)
            refs = self.via_y(p, cf, nx)
            self.tx[f'ry{k}'] = remote(zip(refs, refs), Y)
            refs = self.whole(p, cf)
            self.tx[f'c{k}'] = remote(zip(refs, refs), C)

        def got_y(self, k):
            arrive(self.tx[f'y{k}'])
            refs = self.via_x(self.plane(k), f2, cx)
            self.tx[f'rx{k}'] = remote(zip(refs, refs), X)

        def got_r(self, k):
            arrive(self.tx[f'rx{k}'])
            arrive(self.tx[f'ry{k}'])
            refs = self.whole(self.plane(k), f2)
            self.tx[f'd{k}'] = remote(zip(refs, refs), C)

        def done(self, k):
            arrive(self.tx[f'c{k}'])
            arrive(self.tx[f'd{k}'])

    def local(src, dst, n):
        cp = pltpu.make_async_copy(src, dst, loc_sems.at[n])
        cp.start()
        return cp

    grp = {(kind, l): Group(kind, l) for kind in 'qom' for l in range(2)}
    q0, o0, m0, q1, o1, m1 = [grp[k] for k in (('q', 0), ('o', 0), ('m', 0), ('q', 1), ('o', 1), ('m', 1))]

    q0.begin_plane()
    o0.begin_ring()
    o0.begin_plane()
    gain_tx = []
    for off in range(1, 4):
        gain_tx.append(remote([(gain_ref, gp.at[cf])], (cx, cz, (cf + off) % 4)))
    ld_x = local(x_ref, xbuf, 0)
    ld_g = local(gain_ref, gp.at[cf], 1)
    ld_t = local(tab_ref, cosb, 2)
    ld_h = local(x_ref.at[rows(cz * chunk, chunk), :], hb, 3)
    ld_t.wait()

    def make_tables(i):
        r = rows(i * 256, 256)
        tab = cosb[r, :]
        rolled = pltpu.roll(tab, 64, 1)
        low = lax.broadcasted_iota(jnp.int32, (256, 128), 1) < 64
        cosb[r, :] = jnp.where(low, tab, rolled)
        sinb[r, :] = jnp.where(low, -rolled, tab)

    loop(seq // 256, make_tables)

    o0.got_z(1)
    o0.got_z(2)
    q0.got_y0()
    o0.got_z(3)
    m0.begin_ring()
    m0.begin_plane()
    o0.got_y0()
    q0.got_rx0()
    for tx in gain_tx:
        arrive(tx)
    q0.done(0)
    ld_x.wait()
    ld_g.wait()
    ld_h.wait()

    def gain_row(i):
        return jnp.concatenate([gp[f, i:i + 1, :] for f in range(4)], axis=1)

    def front(layer, wqkv, raw, qkv, obuf, ag_tx, ticks):
        loads = [local(aq_ref.at[layer, i, rows(((cf + j) % 4) * 512, 512), :],
                       wqkv.at[i, rows(((cf + j) % 4) * 512, 512), :], 4 + i * 4 + j) for i in range(3) for j in range(1, 4)]
        loads += [local(r.at[layer], wqkv.at[i, rows(cf * 512, 512), :], 4 + i * 4)
                  for i, r in enumerate((wq_ref, wk_ref, wv_ref))]
        for cp in loads:
            cp.wait()
        lane = lax.broadcasted_iota(jnp.int32, (256, 128), 1)

        def project(t):
            r = rows(t * 256, 256)
            xt = xbuf[r, :]
            qv = dot_nn(xt, wqkv[0])
            raw[0, r, :] = qv
            kv = dot_nn(xt, wqkv[1])
            raw[1, r, :] = kv
            qkv[2, r, :] = dot_nn(xt, wqkv[2]).astype(BF16)
            qs = jnp.sum(qv * qv, axis=-1, keepdims=True)
            ks = jnp.sum(kv * kv, axis=-1, keepdims=True)
            both = jnp.where(lane == 0, qs, jnp.where(lane == 1, ks, 0.0))
            sqb[layer, cz, :, pl.ds(pl.multiple_of(t * 256, 256), 256)] = both.T[0:8, :]

        if ag_tx is None:
            loop(seq // 256, project)
        else:
            for s in range(4):
                ag_tx(s)
                base = ((cz + 4 - s) % 4) * 2
                loop(2, lambda t: project(base + t))
        sq_tx = []
        for off in range(1, 4):
            ref = sqb.at[layer, cz]
            sq_tx.append(remote([(ref, ref)], (cx, (cz + off) % 4, cf)))
        cp_v = local(qkv.at[2], vc_ref.at[layer], 20)
        ticks[0]()
        for tx in sq_tx:
            arrive(tx)

        def rope(t):
            r = rows(t * 256, 256)
            c = pl.ds(pl.multiple_of(t * 256, 256), 256)
            tot = sqb[layer, 0, :, c] + sqb[layer, 1, :, c] + sqb[layer, 2, :, c] + sqb[layer, 3, :, c]
            inv = lax.rsqrt(tot * (1.0 / (4 * 512)) + NORM_EPS)
            cols = jnp.concatenate([inv] * 16, axis=0).T
            cos_t, sin_t = cosb[r, :], sinb[r, :]
            for i in range(2):
                scale = cols[:, i:i + 1]
                for h in range(4):
                    hs = slice(h * 128, (h + 1) * 128)
                    val = raw[i, r, hs] * scale * gp[cf, 4 + 2 * i + layer:5 + 2 * i + layer, hs]
                    qkv[i, r, hs] = (val * cos_t + pltpu.roll(val, 64, 1) * sin_t).astype(BF16)

        loop(seq // 256, rope)
        cp_k = local(qkv.at[1], kc_ref.at[layer], 21)
        ticks[1]()
        order = (2, 1, 3, 0)
        bq = 256
        sm = (HEAD_DIM ** -0.5) * LOG2E
        o_tx = []

        def attend(off):
            j = (cz + off) % 4

            def step(it):
                h, sub = it // 2, it % 2
                i = 2 * j + sub
                hc = pl.ds(pl.multiple_of(h * 128, 128), 128)
                for n in range(seq // bq):
                    @pl.when(i == n)
                    def _():
                        q_blk = qkv[0, n * bq:(n + 1) * bq, hc]
                        diag = dot_nt(q_blk, qkv[1, n * bq:(n + 1) * bq, hc])
                        ri = lax.broadcasted_iota(jnp.int32, (bq, bq), 0)
                        ci = lax.broadcasted_iota(jnp.int32, (bq, bq), 1)
                        diag = jnp.where(ri >= ci, diag, -jnp.inf)
                        top = jnp.max(diag, axis=-1, keepdims=True)
                        if n:
                            full = dot_nt(q_blk, qkv[1, 0:n * bq, hc])
                            top = jnp.maximum(top, jnp.max(full, axis=-1, keepdims=True))
                        e_diag = jnp.exp2((diag - top) * sm)
                        total = jnp.sum(e_diag, axis=-1, keepdims=True)
                        if n:
                            e_full = jnp.exp2((full - top) * sm)
                            total = total + jnp.sum(e_full, axis=-1, keepdims=True)
                        inv = 1.0 / total
                        out = dot_nn((e_diag * inv).astype(BF16), qkv[2, n * bq:(n + 1) * bq, hc])
                        if n:
                            out = out + dot_nn((e_full * inv).astype(BF16), qkv[2, 0:n * bq, hc])
                        obuf[n * bq:(n + 1) * bq, hc] = out.astype(BF16)

            loop(8, step)

        def attend_all(g):
            off = jnp.where(g == 0, 2, jnp.where(g == 1, 1, jnp.where(g == 2, 3, 0)))
            attend(off)
            for gi, o in enumerate(order[:3]):
                @pl.when(g == gi)
                def _():
                    o_tx[gi].start()

        for o in order[:3]:
            n = state['n']
            state['n'] = n + 1
            j = (cz + o) % 4
            cp = pltpu.make_async_remote_copy(
                src_ref=obuf.at[rows(j * chunk, chunk), :],
                dst_ref=ofull.at[layer, :, pl.ds(pl.multiple_of(cz * 512, 512), 512)],
                send_sem=send_sems.at[n], recv_sem=recv_sems.at[n], device_id=(cx, j, cf), device_id_type=MESH)
            o_tx.append(cp)
        loop(4, attend_all)
        ofull[layer, :, pl.ds(pl.multiple_of(cz * 512, 512), 512)] = obuf[rows(cz * chunk, chunk), :]
        ticks[2]()
        cp_v.wait()
        cp_k.wait()
        for cp in o_tx:
            cp.wait_send()
            cp.wait_recv()

    def proj(layer, wo):
        loads = []
        for p in range(4):
            for f in range(4):
                n = 4 + p * 4 + f
                mine = jnp.logical_and(cz == p, cf == f)

                @pl.when(mine)
                def _():
                    local(wo_ref.at[layer], wo.at[p, f], n)

                @pl.when(jnp.logical_not(mine))
                def _():
                    local(ao_ref.at[layer, p, f], wo.at[p, f], n)
                loads.append(pltpu.make_async_copy(wo_ref.at[layer], wo.at[p, f], loc_sems.at[n]))
        for cp in loads:
            cp.wait()
        gain = gain_row(layer)

        def tile(t):
            r = rows(t * 256, 256)
            ot = ofull[layer, r, :]
            parts = []
            for f in range(4):
                acc = dot_nn(ot[:, 0:512], wo[0, f])
                for p in range(1, 4):
                    acc = acc + dot_nn(ot[:, p * 512:(p + 1) * 512], wo[p, f])
                parts.append(acc.astype(BF16).astype(F32))
            a = jnp.concatenate(parts, axis=1)
            scale = lax.rsqrt(jnp.mean(a * a, axis=-1, keepdims=True) + NORM_EPS)
            hb[r, :] = (hb[r, :].astype(F32) + a * scale * gain).astype(BF16)

        loop(2, tile)

    def mlp(layer, gbuf, ubuf, dbuf, acc, ready, after, finish):
        pend = {}

        def fetch(k):
            s = k % 2
            p = grp[('m', layer)].plane(k)
            cps = []
            base = 4 + s * 12
            for j in range(4):
                f = (cf + j) % 4
                r = rows(f * 512, 512)
                own = k == 0 and j == 0
                g_src = wg_ref.at[layer] if own else ag_ref.at[layer, p, r, :]
                u_src = wu_ref.at[layer] if own else au_ref.at[layer, p, r, :]
                d_src = wd_ref.at[layer] if own else ad_ref.at[layer, p, f]
                cps.append(local(g_src, gbuf.at[s, r, :], base + j))
                cps.append(local(u_src, ubuf.at[s, r, :], base + 4 + j))
                cps.append(local(d_src, dbuf.at[s, f], base + 8 + j))
            pend[k] = cps

        ready(0)
        fetch(0)
        for k in range(4):
            if k < 3 and layer == 1:
                ready(k + 1)
                fetch(k + 1)
            for cp in pend[k]:
                cp.wait()
            s = k % 2

            def tile(t):
                r = rows(t * 256, 256)
                ht = hb[r, :]
                gate = dot_nn(ht, gbuf[s])
                up = dot_nn(ht, ubuf[s])
                act = (jax.nn.silu(gate) * up).astype(BF16)
                for f in range(4):
                    c = slice(f * 512, (f + 1) * 512)
                    val = dot_nn(act, dbuf[s, f])
                    if k:
                        val = val + acc[r, c]
                    acc[r, c] = val
                if k == 3:
                    m = acc[r, :].astype(BF16).astype(F32)
                    scale = lax.rsqrt(jnp.mean(m * m, axis=-1, keepdims=True) + NORM_EPS)
                    hb[r, :] = (hb[r, :].astype(F32) + m * scale * gain_row(2 + layer)).astype(BF16)

            if k < 3:
                loop(2, tile)
                after(k)
                if layer == 0:
                    ready(k + 1)
                    fetch(k + 1)
            else:
                for t in range(2):
                    tile(t)
                    finish(t)

    front_scope = dict(wqkv=pltpu.VMEM((3, seq, 512), BF16), raw=pltpu.VMEM((2, seq, 512), F32),
                       qkv=pltpu.VMEM((3, seq, 512), BF16), obuf=pltpu.VMEM((seq, 512), BF16))
    mlp_scope = dict(gbuf=pltpu.VMEM((2, 2048, 1376), BF16), ubuf=pltpu.VMEM((2, 2048, 1376), BF16),
                     dbuf=pltpu.VMEM((2, 4, 1376, 512), BF16), acc=pltpu.VMEM((chunk, 2048), F32))

    def nothing():
        pass

    def tick_a():
        for k in range(1, 4):
            o0.got_x(k)
            o0.got_y(k)
        o0.got_rx0()

    def tick_b():
        m0.got_z(1)
        for k in range(1, 4):
            o0.got_r(k)

    def tick_c():
        m0.got_y0()
        for k in range(4):
            o0.done(k)

    pl.run_scoped(lambda **kw: front(0, ag_tx=None, ticks=(tick_a, tick_b, tick_c), **kw), **front_scope)
    m0.got_z(2)
    pl.run_scoped(lambda wo: proj(0, wo), pltpu.VMEM((4, 4, 512, 512), BF16))
    m0.got_x(1)
    m0.got_y(1)

    def ready0(k):
        if k == 0:
            m0.got_z(3)
            m0.got_rx0()
            m0.got_x(2)
            m0.got_y(2)
        if k == 1:
            m0.got_r(1)
        if k == 2:
            m0.got_x(3)
            m0.got_y(3)
            q1.begin_plane()
            o1.begin_plane()
            m1.begin_plane()
            m0.got_r(2)
        if k == 3:
            m0.got_r(3)
        m0.done(k)

    def after0(k):
        if k == 0:
            o1.begin_ring()
            m1.begin_ring()
        if k == 1:
            o1.got_z(1)
            o1.got_z(2)

    ag = {}

    def finish0(t):
        blk = rows(cz * chunk + t * 256, 256)
        ag[(0, t)] = remote([(hb.at[rows(t * 256, 256), :], xbuf.at[blk, :])], Z)
        xbuf[blk, :] = hb[rows(t * 256, 256), :]

    pl.run_scoped(lambda **kw: mlp(0, ready=ready0, after=after0, finish=finish0, **kw), **mlp_scope)

    def ag_step(s):
        if s == 0:
            q1.got_y0()
            o1.got_z(3)
            o1.got_y0()
            q1.got_rx0()
            q1.done(0)
            return
        for t in range(2):
            arrive(ag[(s - 1, t)])
            if s < 3:
                blk = rows(((cz + 4 - s) % 4) * chunk + t * 256, 256)
                ag[(s, t)] = remote([(xbuf.at[blk, :], xbuf.at[blk, :])], Z)
        if s == 1:
            m1.got_z(1)
            for k in range(1, 4):
                o1.got_x(k)
                o1.got_y(k)
            o1.got_rx0()
            m1.got_y0()
        if s == 2:
            for k in range(1, 4):
                o1.got_r(k)
            m1.got_x(1)
            m1.got_y(1)
            m1.got_z(2)

    def tick_d():
        m1.got_rx0()

    def tick_f():
        for k in range(4):
            o1.done(k)
        m1.got_r(1)
        m1.got_z(3)

    def front_one(**kw):
        ag_step(0)
        front(1, ag_tx=lambda s: ag_step(s) if s else None, ticks=(tick_d, nothing, tick_f), **kw)

    pl.run_scoped(front_one, **front_scope)
    for s in range(3):
        for t in range(2):
            flush(ag[(s, t)][0])
    pl.run_scoped(lambda wo: proj(1, wo), pltpu.VMEM((4, 4, 512, 512), BF16))

    def ready1(k):
        if k == 0:
            m1.got_x(2)
            m1.got_y(2)
        if k == 2:
            m1.got_x(3)
            m1.got_y(3)
            m1.got_r(2)
        if k == 3:
            m1.got_r(3)
        m1.done(k)

    fin = {}

    def finish1(t):
        blk = rows(cz * chunk + t * 256, 256)
        fin[(0, t)] = remote([(hb.at[rows(t * 256, 256), :], y_ref.at[blk, :])], Z)
        local(hb.at[rows(t * 256, 256), :], y_ref.at[blk, :], 1 + t)

    pl.run_scoped(lambda **kw: mlp(1, ready=ready1, after=lambda k: None, finish=finish1, **kw), **mlp_scope)
    for s in range(1, 4):
        for t in range(2):
            arrive(fin[(s - 1, t)])
            if s < 3:
                blk = rows(((cz + 4 - s) % 4) * chunk + t * 256, 256)
                fin[(s, t)] = remote([(y_ref.at[blk, :], y_ref.at[blk, :])], Z)
    for t in range(2):
        pltpu.make_async_copy(hb.at[rows(t * 256, 256), :], y_ref.at[rows(t * 256, 256), :], loc_sems.at[1 + t]).wait()
    waited = {id(ag[(s, t)][0]) for s in range(3) for t in range(2)}
    for cp in sent:
        if id(cp) not in waited:
            flush(cp)
    assert state['n'] <= N_SEM


def mega_call(x, wq, wk, wv, wo, wg, wu, wd, gains, tab):
    seq, width = x.shape
    any_spec = pl.BlockSpec(memory_space=pl.ANY)
    chunk = seq // 4
    outs = [jax.ShapeDtypeStruct((seq, width), BF16),
            jax.ShapeDtypeStruct((2, seq, 512), BF16), jax.ShapeDtypeStruct((2, seq, 512), BF16),
            jax.ShapeDtypeStruct((2, 3, 2048, 512), BF16), jax.ShapeDtypeStruct((2, 4, 4, 512, 512), BF16),
            jax.ShapeDtypeStruct((2, 4, 2048, 1376), BF16), jax.ShapeDtypeStruct((2, 4, 2048, 1376), BF16),
            jax.ShapeDtypeStruct((2, 4, 4, 1376, 512), BF16)]
    return pl.pallas_call(
        mega,
        in_specs=[any_spec] * 10,
        out_specs=[any_spec] * 8,
        out_shape=outs,
        scratch_shapes=[pltpu.VMEM((seq, width), BF16), pltpu.VMEM((chunk, width), BF16),
                        pltpu.VMEM((2, chunk, width), BF16), pltpu.VMEM((2, 4, 8, seq), F32),
                        pltpu.VMEM((seq, 128), F32), pltpu.VMEM((seq, 128), F32), pltpu.VMEM((4, 8, 512), F32),
                        pltpu.SemaphoreType.DMA((N_SEM,)), pltpu.SemaphoreType.DMA((N_SEM,)),
                        pltpu.SemaphoreType.DMA((32,))],
        compiler_params=pltpu.CompilerParams(has_side_effects=True, vmem_limit_bytes=67043328),
        name='mega')(x, wq, wk, wv, wo, wg, wu, wd, gains, tab)


def solution(mesh):
    batch_axes = ('dp', 'fsdp')
    act_spec = P(batch_axes, None, None)
    in_cols = P(None, 'fsdp', 'tp')
    in_rows = P(None, 'tp', 'fsdp')
    tp_gain = P(None, 'tp')
    fsdp_gain = P(None, 'fsdp')
    cache_spec = P(None, batch_axes, None, 'tp', None)

    def local_layers(x, w_query, w_key, w_value, w_out, w_gate, w_up, w_down, q_norm_w, k_norm_w, attn_norm_w, ffn_norm_w):
        batch, seq_len, width = x.shape
        gains = jnp.concatenate([attn_norm_w, ffn_norm_w, q_norm_w, k_norm_w], axis=0)
        tab = jnp.asarray(rope_table(seq_len))
        outs = mega_call(x.reshape(seq_len, width), w_query, w_key, w_value, w_out, w_gate, w_up, w_down, gains, tab)
        shape = (2, 1, seq_len, 4, HEAD_DIM)
        return outs[0].reshape(x.shape), outs[1].reshape(shape), outs[2].reshape(shape)

    return jax.shard_map(local_layers, mesh=mesh,
                         in_specs=(act_spec, in_cols, in_cols, in_cols, in_rows, in_cols, in_cols, in_rows,
                                   tp_gain, tp_gain, fsdp_gain, fsdp_gain),
                         out_specs=(act_spec, cache_spec, cache_spec), check_vma=False)
```

time: 1940 us -> 986 us (0.51)
  waiting for transfers between devices: 1320 us -> 0 us
  Pallas kernels: 0 us -> 945 us
  matrix products: 337 us -> 0 us
  other arithmetic: 107 us -> 1.51 us
  blocking collectives: 58.6 us -> 0 us
  local copies, waits for them, and re-layouts: 85.4 us -> 29.4 us
    psum x4 -> x0, waiting for transfers between devices: 1080 us -> none  [the longest x2 550 us: local_layers(): a_out = lax.psum(a_part, 'tp').astype(jnp.float32)]
    pallas_call x0 -> x1, Pallas kernels: none -> 945 us  [mega_call(): pl.pallas_call(mega, in_specs=[any_spec] * 10, out_specs=[any_spec] * 8,...]
    dot_general x14 -> x0, matrix products: 269 us -> none  [the longest x2 77.5 us: attend(): jnp.einsum('bhqk,bkhd->bqhd', attn_probs, values, preferred_element_type=...]
    all_gather x14 -> x0, waiting for transfers between devices: 243 us -> none  [the longest x2 88.8 us: local_layers(): wd_full = lax.all_gather(w_down[layer], 'fsdp', axis=1, tiled=True)]
    sub x2 -> x0, matrix products: 67.4 us -> none  [attend(): attn_probs = jax.nn.softmax(scores, axis=-1).astype(jnp.bfloat16)]
    unnamed x53 -> x5, local copies, waits for them, and re-layouts: 53.7 us -> 15.7 us
    psum x2 -> x0, blocking collectives: 38 us -> none  [local_layers(): sq_total = lax.psum(sq_local, 'tp')]
    convert_element_type x3 -> x0, other arithmetic: 28 us -> none  [the longest x2 18.6 us: local_layers(): (hidden.astype(jnp.float32) + a_out * rms_scale(a_out) * attn_gain).astyp...]
  transfers between devices with their start and end apart: 18 -> 0, of which waited for: 14 -> 0; matrix products, arithmetic and copies ran while one was open for 22% -> 0% of each run, Pallas kernels for 0% -> 0%
where the time goes in v1:
time: 986 us; the launch traced here: 977 us
  Pallas kernels  945 us (96%)
  local copies, waits for them, and re-layouts  29.4 us (3%)
    pallas_call x1, Pallas kernels, mega_call(): pl.pallas_call(mega, in_specs=[any_spec] * 10, out_specs=[any_spec] * 8,...  945 us

profile of v1, /device:TPU:0, one launch (start us, length us, event | category | flops | bytes accessed | tf_op | source)
XLA Modules:
  0.0 977.1 jit_solution(4971085056427168314)
XLA Ops:
  0.6 0.0 copy-start
  0.6 1.5 pad_maximum_fusion.gain_ref
  2.1 4.5 copy.16.wg_ref
  6.7 0.0 copy-done
  6.7 2.7 copy.17.wu_ref
  9.4 945.1 %mega.1 = (bf16[2048,2048]{1,0:T(8,128)(2,1)}, bf16[2,2048,512]{2,1,0:T(8,128)(2,1)}, bf16[2,2048,512]{2,1,0:T(8,128)(2,1)}, bf16[2,3,2048,512]{3,2,1,0:T(8,128)...) custom-call(bf16[2048,2048]{1,0:T(8,128)(2,1)} %bitcast.4, ...), custom_call_target="tpu_custom_call" | custom-call | tf_op jit(solution)/shard_map/mega/pallas_call | solution.py:609
  954.5 6.9 reshape.20
  961.3 6.9 reshape.21
  968.2 8.4 copy.21
Async XLA Ops:
  0.6 6.0 copy-start

commit v2 on v0

v2 whole, which is shorter than its diff:
```python
import functools
import jax
import jax.numpy as jnp
import numpy as np
from jax import lax
from jax.experimental import pallas as pl
from jax.experimental.pallas import tpu as pltpu
from jax.sharding import PartitionSpec as P

HEAD_DIM = 128
NORM_EPS = 1e-6
ROPE_THETA = 500000.0
LOG2E = 1.4426950408889634
MESH = pl.DeviceIdType.MESH
BF16 = jnp.bfloat16
F32 = jnp.float32
N_SEM = 300
TILE = 256
BLK = 512
LANE = 128
F_HALF = 688
S1, S2, S3 = SLOTS = (1, 2, 3)
PAIR = range(2)
TRIO = range(3)
QUAD = range(4)
ALL = slice(None)


def rope_table(seq_len):
    half = HEAD_DIM // 2
    inv_freq = np.float32(ROPE_THETA) ** (-2.0 * np.arange(half, dtype=np.float32) / np.float32(HEAD_DIM))
    angles = np.arange(seq_len, dtype=np.float32)[:, None] * inv_freq.astype(np.float32)[None, :]
    return np.concatenate([np.cos(angles), np.sin(angles)], axis=1).astype(np.float32)


def dot_nt(lhs, rhs):
    return lax.dot_general(lhs, rhs, (((1,), (1,)), ((), ())), preferred_element_type=F32)


def dot_nn(lhs, rhs):
    return jnp.dot(lhs, rhs, preferred_element_type=F32)


def loop(count, body):
    lax.fori_loop(0, count, lambda i, c: (body(i), c)[1], 0)


def mega(x_ref, wq_ref, wk_ref, wv_ref, wo_ref, wg_ref, wu_ref, wd_ref, gain_ref, tab_ref,
         y_ref, kc_ref, vc_ref, aq_ref, ao_ref, aw_ref, bw_ref,
         xbuf, hb, mrecv, ofull, sqb, cosb, sinb, gp, send_sems, recv_sems, loc_sems):
    seq = x_ref.shape[0]
    chunk = seq // 4
    cx, cz, cf = lax.axis_index('dp'), lax.axis_index('tp'), lax.axis_index('fsdp')
    cy = cf // 2
    f1 = cf + 1 - 2 * (cf % 2)
    f2 = (cf + 2) % 4
    nx = 1 - cx
    X = (nx, cz, cf)
    Y = (cx, cz, f2)
    C = (cx, cz, f1)
    mid = (cz + 1) // 2 == 1
    half_z = cz // 2
    outer = 3 * half_z
    state = {'send': 0, 'recv': 0}
    sent = []

    def take_number(kind):
        state[kind] += 1
        return state[kind] - 1

    def frozen(ref):
        if not getattr(ref, 'transforms', ()):
            return ref, None
        idx, = ref.transforms
        return ref.ref, tuple(int(i.size) if isinstance(i, pl.Slice) else None for i in idx.indices)

    def thawed(item):
        ref, sizes = item
        return ref if sizes is None else ref.at[tuple(0 if s is None else pl.ds(0, s) for s in sizes)]

    def expect(pairs):
        return [(take_number('recv'), frozen(dst)) for _, dst in pairs]

    def remote(pairs, dev, into=None, when=None):
        pairs = list(pairs)
        into = expect(pairs) if into is None else into
        for (src, dst), (n, _) in zip(pairs, into):
            m = take_number('send')
            cp = pltpu.make_async_remote_copy(src_ref=src, dst_ref=dst, send_sem=send_sems.at[m], recv_sem=recv_sems.at[n],
                                              device_id=dev, device_id_type=MESH)
            cp.start()
            sent.append((m, frozen(src), when))
        return into

    def handle(ref, m, n):
        return pltpu.make_async_remote_copy(src_ref=thawed(ref), dst_ref=thawed(ref), send_sem=send_sems.at[m],
                                            recv_sem=recv_sems.at[n], device_id=(0, 0, 0), device_id_type=MESH)

    def arrive(cps, name='recv'):
        with jax.named_scope(name):
            for n, ref in cps:
                handle(ref, 0, n).wait_recv()

    def flush(first=0, last=None):
        for m, ref, when in sent[first:last]:
            if m in flushed:
                continue
            flushed.add(m)
            if when is None:
                handle(ref, m, 0).wait_send()
            else:
                @pl.when(mid if when == 'mid' else jnp.logical_not(mid))
                def _():
                    handle(ref, m, 0).wait_send()

    flushed = set()

    def slot_plane(k):
        return (cz, 1 - cz + 4 * half_z, 2 - half_z, 3 - 3 * half_z)[k]

    class Cast:
        def __init__(self, name):
            self.name, self.slots, self.heard = name, None, set()

        def push(self, k, pairs):
            pairs = list(pairs)
            if self.slots is None:
                self.slots = [None] + [expect(pairs) for _ in TRIO]

            @pl.when(mid)
            def _():
                if k < 2:
                    remote(pairs, (cx, 3 - cz, cf), self.slots[2 + k], 'mid')
                if k != 1:
                    remote(pairs, (cx, outer, cf), self.slots[max(k, 1)], 'mid')
            if k == 0:
                @pl.when(jnp.logical_not(mid))
                def _():
                    remote(pairs, (cx, 1 + half_z, cf), self.slots[1], 'end')

        def hear(self, k):
            if k not in self.heard:
                self.heard.add(k)

                @pl.when(mid)
                def _():
                    arrive(self.slots[k], f'relay_{self.name}_{k}')

        def relay(self, k, pairs):
            self.hear(k)
            self.push(k, pairs)

        def take(self, k):
            self.hear(k)

            @pl.when(jnp.logical_not(mid))
            def _():
                arrive(self.slots[k], f'take_{self.name}_{k}')

    def rows(base, size):
        return pl.ds(base if isinstance(base, int) else pl.multiple_of(base, 16), size)

    def cols(base, size):
        return pl.ds(base if isinstance(base, int) else pl.multiple_of(base, LANE), size)

    def same(refs):
        return list(zip(refs, refs))

    class Group:
        def __init__(self, kind, layer):
            self.kind, self.layer, self.tx = kind, layer, {}

        def plane(self, k):
            return slot_plane(k)

        def cast(self, key):
            name = f'{self.kind}{self.layer}{key}'
            return self.tx.setdefault('cast' + key, Cast(name))

        def wait(self, *keys):
            for key in keys:
                arrive(self.tx[key], f'wait_{self.kind}{self.layer}_{key}')

        def send(self, key, pairs, dev):
            self.tx[key] = remote(pairs, dev)

    class QGroup(Group):
        def whole(self, i, f):
            return aq_ref.at[self.layer, i, rows(f * BLK, BLK), :]

        def half(self, i, f):
            return aq_ref.at[self.layer, i, rows(f * BLK + cx * TILE, TILE), :]

        def begin(self):
            own = (wq_ref, wk_ref, wv_ref)
            for i in TRIO:
                self.send(f'y{i}', [(own[i].at[self.layer, rows(cx * TILE, TILE), :], self.half(i, cf))], Y)
            for i in TRIO:
                self.send(f'c{i}', [(own[i].at[self.layer], self.whole(i, cf))], C)

        def got_y(self, i):
            self.wait(f'y{i}')
            self.send(f'r{i}', same([self.half(i, f2)]), X)

        def got_r(self, i):
            self.wait(f'r{i}')
            self.send(f'd{i}', same([self.whole(i, f2)]), C)

        def done(self):
            for i in TRIO:
                self.wait(f'c{i}', f'd{i}')

    class OGroup(Group):
        def whole(self, p, f):
            return ao_ref.at[self.layer, p, f]

        def part(self, p, f, first, size):
            return ao_ref.at[self.layer, p, f, rows(first, size), :]

        def begin(self):
            half = self.part(cz, cf, cx * TILE, TILE)
            src = wo_ref.at[self.layer, rows(cx * TILE, TILE), :]
            self.cast('').push(0, [(src, half)])

        def begin_y(self):
            own, half = wo_ref.at[self.layer], self.part(cz, cf, cx * TILE, TILE)
            src = wo_ref.at[self.layer, rows(cx * TILE, TILE), :]
            self.send('y0', [(src, half)], Y)
            self.send('c0', [(own, self.whole(cz, cf))], C)

        def got_y0(self):
            self.wait('y0')
            self.send('rx0', same([self.part(cz, f2, cx * TILE, TILE)]), X)

        def got_rx0(self):
            self.wait('rx0')
            self.send('d0', same([self.whole(cz, f2)]), C)

        def relay(self, k):
            self.cast('').relay(k, same([self.part(self.plane(k), cf, cx * TILE, TILE)]))

        def take(self, k):
            self.cast('').take(k)
            refs = same([self.part(self.plane(k), cf, cx * TILE, TILE)])
            self.send(f'x{k}', refs, X)
            self.send(f'y{k}', refs, Y)

        def got_xy(self, k):
            p = self.plane(k)
            self.wait(f'x{k}')
            self.send(f'ry{k}', same([self.part(p, cf, nx * TILE + LANE, LANE)]), Y)
            self.send(f'c{k}', same([self.whole(p, cf)]), C)
            self.wait(f'y{k}')
            self.send(f'rx{k}', same([self.part(p, f2, cx * TILE, LANE)]), X)

        def got_r(self, k):
            self.wait(f'rx{k}', f'ry{k}')
            self.send(f'd{k}', same([self.whole(self.plane(k), f2)]), C)

        def done(self):
            for k in QUAD:
                self.wait(f'c{k}', f'd{k}')

    class MGroup(Group):
        def whole(self, p, f):
            return aw_ref.at[p, f]

        def lane(self, p, f, i):
            return aw_ref.at[p, f, i, :, cols(cx * TILE, TILE)]

        def first(self, f, xh, own_y, i):
            src = (wg_ref, wu_ref, wd_ref)[i].at[self.layer, rows(own_y * F_HALF, F_HALF), cols(xh * TILE, TILE)]
            return src, aw_ref.at[cz, f, i, :, cols(xh * TILE, TILE)]

        def begin_ring(self):
            self.cast('a').push(0, [self.first(cf, cx, cy, i) for i in TRIO])

        def begin_y(self):
            self.send('ya', [self.first(cf, cx, 1 - cy, i) for i in TRIO], Y)

        def begin_y_rest(self):
            self.send('yb', [self.first(cf, nx, 1 - cy, i) for i in TRIO], Y)

        def begin_c(self):
            self.send('c0', [((wg_ref, wu_ref, wd_ref)[i].at[self.layer, rows(cy * F_HALF, F_HALF), :], aw_ref.at[cz, cf, i])
                             for i in TRIO], C)

        def got_ya(self):
            self.wait('ya')
            self.cast('b').push(0, same([self.lane(cz, f2, i) for i in TRIO]))

        def got_yb(self):
            self.wait('yb')
            self.send('d0', same([self.whole(cz, f2)]), C)

        def relay(self, ab, k):
            f = cf if ab == 'a' else f2
            self.cast(ab).relay(k, same([self.lane(self.plane(k), f, i) for i in TRIO]))

        def take(self, ab, k):
            self.cast(ab).take(k)
            f = cf if ab == 'a' else f2
            self.send(f'x{ab}{k}', same([self.lane(self.plane(k), f, i) for i in TRIO]), X)

        def got_x(self, ab, k):
            self.wait(f'x{ab}{k}')
            self.send(f"{'c' if ab == 'a' else 'd'}{k}", same([self.whole(self.plane(k), cf if ab == 'a' else f2)]), C)

        def done(self, k):
            self.wait(f'c{k}', f'd{k}')

    class WideGroup(Group):
        def srcs(self):
            return [r.at[self.layer, rows(cx * F_HALF, F_HALF), :] for r in (wg_ref, wu_ref, wd_ref)]

        def block(self, p, f, i):
            return bw_ref.at[p, f, i]

        def half(self, p, f, xh, i):
            return bw_ref.at[p, f, i, rows(xh * F_HALF, F_HALF), :]

        def quarter(self, p, f, xh, i, side):
            return bw_ref.at[p, f, i, rows(xh * F_HALF, F_HALF), pl.ds(side * TILE, TILE)]

        def begin_ring(self, i):
            self.cast(f'{i}').push(0, [(self.srcs()[i], self.half(cz, cf, cx, i))])

        def begin_y(self):
            for i in TRIO:
                self.send(f'y0{i}', [(self.srcs()[i], self.half(cz, cf, cx, i))], Y)

        def begin_c(self):
            own = [r.at[self.layer] for r in (wg_ref, wu_ref, wd_ref)]
            self.send('c0', [(own[i], self.block(cz, cf, i)) for i in TRIO], C)

        def got_y0(self, i):
            self.wait(f'y0{i}')
            self.send(f'r0{i}', same([self.half(cz, f2, cx, i)]), X)

        def got_r0(self):
            self.wait('r00', 'r01', 'r02')
            self.send('d0', same([bw_ref.at[cz, f2]]), C)

        def relay(self, k, i):
            self.cast(f'{i}').relay(k, same([self.half(self.plane(k), cf, cx, i)]))

        def take(self, k, i, spread=True):
            self.cast(f'{i}').take(k)
            self.send(f'x{k}{i}', same([self.half(self.plane(k), cf, cx, i)]), X)
            if spread:
                self.spread(k, i)

        def spread(self, k, i):
            self.send(f'y{k}{i}', same([self.half(self.plane(k), cf, cx, i)]), Y)

        def got_xy(self, k, i):
            p = self.plane(k)
            self.wait(f'x{k}{i}')
            self.send(f'ry{k}{i}', same([self.quarter(p, cf, nx, i, 1)]), Y)
            self.send(f'c{k}{i}', same([self.block(p, cf, i)]), C)
            self.wait(f'y{k}{i}')
            self.send(f'rx{k}{i}', same([self.quarter(p, f2, cx, i, 0)]), X)

        def got_r(self, k, i):
            self.wait(f'rx{k}{i}', f'ry{k}{i}')
            self.send(f'd{k}{i}', same([self.block(self.plane(k), f2, i)]), C)

        def done(self, k):
            if k == 0:
                self.wait('c0', 'd0')
            else:
                for i in TRIO:
                    self.wait(f'c{k}{i}', f'd{k}{i}')

    def local(src, dst, n):
        cp = pltpu.make_async_copy(src, dst, loc_sems.at[n])
        cp.start()
        return cp

    q0, o0, m0 = QGroup('q', 0), OGroup('o', 0), MGroup('m', 0)
    q1, o1, m1 = QGroup('q', 1), OGroup('o', 1), WideGroup('m', 1)

    o0.begin()
    gain_tx = []
    for off in SLOTS:
        gain_tx.append(remote([(gain_ref, gp.at[cf])], (cx, cz, (cf + off) % 4)))
    q0.begin()
    o0.begin_y()
    m0.begin_y()
    m0.begin_c()
    ld_x = local(x_ref, xbuf, 0)
    ld_g = local(gain_ref, gp.at[cf], 1)
    ld_t = local(tab_ref, cosb, 2)
    ld_h = local(x_ref.at[rows(cz * chunk, chunk), :], hb.at[rows(0, chunk), :], 3)
    ld_t.wait()

    def make_tables(i):
        r = rows(i * TILE, TILE)
        tab = cosb[r, :]
        rolled = pltpu.roll(tab, 64, 1)
        low = lax.broadcasted_iota(jnp.int32, (TILE, LANE), 1) < 64
        cosb[r, :] = jnp.where(low, tab, rolled)
        sinb[r, :] = jnp.where(low, -rolled, tab)

    with jax.named_scope('tables'):
        loop(seq // TILE, make_tables)

    o0.relay(1)
    o0.relay(2)
    m0.begin_ring()
    o0.take(1)
    for i in TRIO:
        q0.got_y(i)
    o0.relay(3)
    o0.got_y0()
    for i in TRIO:
        q0.got_r(i)
    for tx in gain_tx:
        arrive(tx)
    q0.done()
    m0.relay('a', 1)
    m0.relay('a', 2)
    ld_x.wait()
    ld_g.wait()
    ld_h.wait()

    def gain_row(i):
        return jnp.concatenate([gp[f, i:i + 1, :] for f in QUAD], axis=1)

    def front(layer, wqkv, raw, qkv, obuf, ag_tx, ticks, mid_hooks):
        loads = [local(aq_ref.at[layer, i, rows(((cf + j) % 4) * BLK, BLK), :],
                       wqkv.at[i, rows(((cf + j) % 4) * BLK, BLK), :], 4 + i * 4 + j) for i in TRIO for j in SLOTS]
        loads += [local(r.at[layer], wqkv.at[i, rows(cf * BLK, BLK), :], 4 + i * 4)
                  for i, r in enumerate((wq_ref, wk_ref, wv_ref))]
        with jax.named_scope('wait_wqkv'):
            for cp in loads:
                cp.wait()
        lane = lax.broadcasted_iota(jnp.int32, (TILE, LANE), 1)

        def project(t):
            r = rows(t * TILE, TILE)
            xt = xbuf[r, :]
            qv = dot_nn(xt, wqkv[0])
            raw[0, r, :] = qv
            kv = dot_nn(xt, wqkv[1])
            raw[1, r, :] = kv
            qkv[2, r, :] = dot_nn(xt, wqkv[2]).astype(BF16)
            qs = jnp.sum(qv * qv, axis=-1, keepdims=True)
            ks = jnp.sum(kv * kv, axis=-1, keepdims=True)
            both = jnp.where(lane == 0, qs, jnp.where(lane == 1, ks, 0.0))
            sqb[layer, cz, :, pl.ds(pl.multiple_of(t * TILE, TILE), TILE)] = both.T[0:8, :]

        if ag_tx is None:
            with jax.named_scope('project'):
                loop(seq // TILE, project)
        else:
            for s in QUAD:
                ag_tx(s)
                base = slot_plane(s) * 2
                with jax.named_scope('project'):
                    loop(2, lambda t: project(base + t))
        sq_tx = []
        for off in SLOTS:
            ref = sqb.at[layer, cz]
            sq_tx.append(remote([(ref, ref)], (cx, (cz + off) % 4, cf)))
        cp_v = local(qkv.at[2], vc_ref.at[layer], 20)
        ticks[0]()
        for tx in sq_tx:
            arrive(tx, 'wait_sq')

        def rope(t):
            r = rows(t * TILE, TILE)
            c = pl.ds(pl.multiple_of(t * TILE, TILE), TILE)
            tot = sqb[layer, 0, :, c] + sqb[layer, 1, :, c] + sqb[layer, 2, :, c] + sqb[layer, 3, :, c]
            inv = lax.rsqrt(tot * (1.0 / (4 * BLK)) + NORM_EPS)
            cols = jnp.concatenate([inv] * 16, axis=0).T
            cos_t, sin_t = cosb[r, :], sinb[r, :]
            for i in PAIR:
                scale = cols[:, i:i + 1]
                for h in QUAD:
                    hs = slice(h * LANE, (h + 1) * LANE)
                    val = raw[i, r, hs] * scale * gp[cf, 4 + 2 * i + layer:5 + 2 * i + layer, hs]
                    qkv[i, r, hs] = (val * cos_t + pltpu.roll(val, 64, 1) * sin_t).astype(BF16)

        with jax.named_scope('rope'):
            loop(seq // TILE, rope)
        cp_k = local(qkv.at[1], kc_ref.at[layer], 21)
        ticks[1]()
        order = (2, 1, 3, 0)
        bq = TILE
        sm = (HEAD_DIM ** -0.5) * LOG2E
        o_tx = []

        def attend(off):
            j = (cz + off) % 4

            def step(it):
                h, sub = it // 2, it % 2
                i = 2 * j + sub
                hc = pl.ds(pl.multiple_of(h * LANE, LANE), LANE)
                for n in range(seq // bq):
                    @pl.when(i == n)
                    def _():
                        q_blk = qkv[0, n * bq:(n + 1) * bq, hc]
                        diag = dot_nt(q_blk, qkv[1, n * bq:(n + 1) * bq, hc])
                        ri = lax.broadcasted_iota(jnp.int32, (bq, bq), 0)
                        ci = lax.broadcasted_iota(jnp.int32, (bq, bq), 1)
                        diag = jnp.where(ri >= ci, diag, -jnp.inf)
                        top = jnp.max(diag, axis=-1, keepdims=True)
                        if n:
                            full = dot_nt(q_blk, qkv[1, 0:n * bq, hc])
                            top = jnp.maximum(top, jnp.max(full, axis=-1, keepdims=True))
                        e_diag = jnp.exp2((diag - top) * sm)
                        total = jnp.sum(e_diag, axis=-1, keepdims=True)
                        if n:
                            e_full = jnp.exp2((full - top) * sm)
                            total = total + jnp.sum(e_full, axis=-1, keepdims=True)
                        inv = 1.0 / total
                        out = dot_nn((e_diag * inv).astype(BF16), qkv[2, n * bq:(n + 1) * bq, hc])
                        if n:
                            out = out + dot_nn((e_full * inv).astype(BF16), qkv[2, 0:n * bq, hc])
                        obuf[n * bq:(n + 1) * bq, hc] = out.astype(BF16)

            loop(8, step)

        def attend_all(g):
            off = jnp.where(g == 0, 2, jnp.where(g == 1, 1, jnp.where(g == 2, 3, 0)))
            attend(off)
            for gi, o in enumerate(order[:3]):
                @pl.when(g == gi)
                def _():
                    o_tx[gi].start()
                    mid_hooks[gi]()

        for o in order[:3]:
            m, n = take_number('send'), take_number('recv')
            j = (cz + o) % 4
            cp = pltpu.make_async_remote_copy(
                src_ref=obuf.at[rows(j * chunk, chunk), :],
                dst_ref=ofull.at[layer, :, pl.ds(pl.multiple_of(cz * BLK, BLK), BLK)],
                send_sem=send_sems.at[m], recv_sem=recv_sems.at[n], device_id=(cx, j, cf), device_id_type=MESH)
            o_tx.append(cp)
        with jax.named_scope('attend'):
            loop(4, attend_all)
        ofull[layer, :, pl.ds(pl.multiple_of(cz * BLK, BLK), BLK)] = obuf[rows(cz * chunk, chunk), :]
        ticks[2]()
        cp_v.wait()
        cp_k.wait()
        with jax.named_scope('wait_o'):
            for cp in o_tx:
                cp.wait_send()
                cp.wait_recv()

    def proj(layer, wo, h_tx):
        loads = []
        for p in QUAD:
            for f in QUAD:
                n = 4 + p * 4 + f
                mine = jnp.logical_and(cz == p, cf == f)

                @pl.when(mine)
                def _():
                    local(wo_ref.at[layer], wo.at[p, f], n)

                @pl.when(jnp.logical_not(mine))
                def _():
                    local(ao_ref.at[layer, p, f], wo.at[p, f], n)
                loads.append(pltpu.make_async_copy(wo_ref.at[layer], wo.at[p, f], loc_sems.at[n]))
        with jax.named_scope('wait_wo'):
            for cp in loads:
                cp.wait()
        gain = gain_row(layer)

        def tile(t):
            r = rows(t * TILE, TILE)
            ot = ofull[layer, r, :]
            parts = []
            for f in QUAD:
                acc = dot_nn(ot[:, 0:BLK], wo[0, f])
                for p in SLOTS:
                    acc = acc + dot_nn(ot[:, p * BLK:(p + 1) * BLK], wo[p, f])
                parts.append(acc.astype(BF16).astype(F32))
            a = jnp.concatenate(parts, axis=1)
            scale = lax.rsqrt(jnp.mean(a * a, axis=-1, keepdims=True) + NORM_EPS)
            hb[r, :] = (hb[r, :].astype(F32) + a * scale * gain).astype(BF16)

        for t in PAIR:
            with jax.named_scope('out_proj'):
                tile(t)
            if layer == 0:
                mark = len(sent)
                h_tx.append((mark, remote([(hb.at[rows(t * TILE, TILE), :], hb.at[rows(chunk + t * TILE, TILE), :])], Y)))

    def mlp_tile(k, t, w, acc, out=None):
        r = rows(t * TILE, TILE)
        ht = hb[r, :]
        gate = dot_nt(ht[:, 0:BLK], w[0, 0])
        up = dot_nt(ht[:, 0:BLK], w[0, 1])
        for f in SLOTS:
            gate = gate + dot_nt(ht[:, f * BLK:(f + 1) * BLK], w[f, 0])
            up = up + dot_nt(ht[:, f * BLK:(f + 1) * BLK], w[f, 1])
        act = (jax.nn.silu(gate) * up).astype(BF16)
        for f in QUAD:
            c = slice(f * BLK, (f + 1) * BLK)
            val = dot_nn(act, w[f, 2])
            if k:
                val = val + acc[r, c]
            if out is None:
                acc[r, c] = val
            else:
                out[rows(t * TILE - chunk, TILE), c] = val.astype(BF16)

    def fetch0(k, wbuf):
        s = k % 2
        p = m0.plane(k)
        cps = []
        for j in QUAD:
            f = (cf + j) % 4
            if k == 0 and j == 0:
                for i, r in enumerate((wg_ref, wu_ref, wd_ref)):
                    cps.append(local(r.at[0, rows(cy * F_HALF, F_HALF), :], wbuf.at[s, f, i], 4 + s * 6 + 3 + i))
            else:
                cps.append(local(aw_ref.at[p, f], wbuf.at[s, f], 4 + s * 6 + (j - 1 if j else 3)))
        return cps

    def fetch1(k, wbuf):
        s = k % 2
        p = m1.plane(k)
        cps = []
        for j in QUAD:
            f = (cf + j) % 4
            if k == 0 and j == 0:
                for i, r in enumerate((wg_ref, wu_ref, wd_ref)):
                    cps.append(local(r.at[1], wbuf.at[s, f, i], 4 + s * 6 + 3 + i))
            else:
                cps.append(local(bw_ref.at[p, f], wbuf.at[s, f], 4 + s * 6 + (j - 1 if j else 3)))
        return cps

    def settle(cps):
        with jax.named_scope('wait_fetch'):
            for cp in cps:
                cp.wait()

    def close(layer, t, m, finish):
        r = rows(t * TILE, TILE)
        m = m.astype(BF16).astype(F32)
        scale = lax.rsqrt(jnp.mean(m * m, axis=-1, keepdims=True) + NORM_EPS)
        hb[r, :] = (hb[r, :].astype(F32) + m * scale * gain_row(2 + layer)).astype(BF16)
        finish(t)

    def mlp0(wbuf, acc, msend, h_tx, ev, finish):
        ev[0]()
        m0.done(0)
        settle(fetch0(0, wbuf))
        with jax.named_scope('mlp0_own'):
            loop(2, lambda t: mlp_tile(0, t, wbuf.at[0], acc))
        ev[7]()
        for _, tx in h_tx:
            arrive(tx, 'wait_h')
        with jax.named_scope('mlp0_other'):
            loop(2, lambda t: mlp_tile(0, t + 2, wbuf.at[0], acc))
        for k in (1, 2):
            ev[k]()
            m0.done(k)
            settle(fetch0(k, wbuf))
            with jax.named_scope('mlp0'):
                loop(4, lambda t: mlp_tile(k, t, wbuf.at[k % 2], acc))
        ev[3]()
        m0.done(3)
        settle(fetch0(3, wbuf))
        m_tx = []
        for t in PAIR:
            with jax.named_scope('mlp0_last'):
                mlp_tile(3, t + 2, wbuf.at[1], acc, msend)
            r = rows(t * TILE, TILE)
            mark = len(sent)
            m_tx.append((mark, remote([(msend.at[r, :], mrecv.at[r, :])], Y)))
        with jax.named_scope('mlp0_own'):
            loop(2, lambda t: mlp_tile(3, t, wbuf.at[1], acc))
        ev[4]()
        for mark, _ in h_tx:
            flush(mark, mark + 1)
        for t in PAIR:
            arrive(m_tx[t][1], f'wait_m_{t}')
            r = rows(t * TILE, TILE)
            close(0, t, acc[r, :] + mrecv[r, :].astype(F32), finish)
            ev[5 + t]()
        for mark, _ in m_tx:
            flush(mark, mark + 1)

    def mlp1(wbuf, acc, ev, finish):
        ev[0]()
        m1.done(0)
        cps = fetch1(0, wbuf)
        for k in QUAD:
            settle(cps)
            if k < 2:
                ev[k + 1]()
                m1.done(k + 1)
                cps = fetch1(k + 1, wbuf)
            if k < 3:
                with jax.named_scope('mlp1'):
                    loop(2, lambda t: mlp_tile(k, t, wbuf.at[k % 2], acc))
                if k == 2:
                    ev[3]()
                    m1.done(3)
                    cps = fetch1(3, wbuf)
            else:
                for t in PAIR:
                    with jax.named_scope('mlp1_last'):
                        mlp_tile(3, t, wbuf.at[1], acc)
                    close(1, t, acc[rows(t * TILE, TILE), :], finish)

    front_scope = dict(wqkv=pltpu.VMEM((3, seq, BLK), BF16), raw=pltpu.VMEM((2, seq, BLK), F32),
                       qkv=pltpu.VMEM((3, seq, BLK), BF16), obuf=pltpu.VMEM((seq, BLK), BF16))
    def nothing():
        pass

    def tick_a():
        m0.got_ya()
        o0.take(S2)
        o0.take(S3)
        m0.take('a', S1)

    def tick_b():
        m0.relay('a', S3)
        o0.got_rx0()

    def mid_a():
        o0.got_xy(S1)
        o0.got_xy(S2)
        m0.take('a', S2)

    def mid_b():
        o0.got_xy(S3)

    def mid_c():
        m0.got_x('a', S1)
        m0.relay('b', S1)
        m0.take('b', S1)

    def tick_c():
        m0.begin_y_rest()
        for k in SLOTS:
            o0.got_r(k)
        o0.done()
        m0.relay('b', S2)

    pl.run_scoped(lambda **kw: front(0, ag_tx=None, ticks=(tick_a, tick_b, tick_c), mid_hooks=(mid_a, mid_b, mid_c), **kw), **front_scope)
    h_tx0 = []
    pl.run_scoped(lambda wo: proj(0, wo, h_tx0), pltpu.VMEM((4, 4, BLK, BLK), BF16))

    def before_own():
        m0.relay('b', S3)
        m0.take('a', S3)
        m0.got_yb()
        m0.got_x('a', S2)
        m0.got_x('b', S1)
        m1.begin_y()
        m1.begin_c()

    def before_other():
        m0.take('b', S2)
        m0.take('b', S3)
        o1.begin()
        for i in TRIO:
            m1.begin_ring(i)
        m0.got_x('a', S3)

    def before_one():
        o1.relay(S1)
        o1.relay(S2)

    def before_two():
        m0.got_x('b', S2)
        o1.relay(S3)

    def before_three():
        m0.got_x('b', S3)
        m1.relay(S1, 0)
        m1.relay(S2, 0)

    def before_sum():
        for i in TRIO:
            m1.got_y0(i)
        m1.take(S1, 0, spread=False)
        for i in TRIO[1:]:
            m1.relay(S2, i)

    def after_first():
        m1.take(S1, TRIO[1], spread=False)

    def after_second():
        q1.begin()
        o1.begin_y()
        m1.take(S1, TRIO[2], spread=False)

    ev0 = (before_own, before_one, before_two, before_three, before_sum, after_first, after_second, before_other)

    ag_marks = []
    ag = [Cast(f'ag_{t}') for t in PAIR]
    fin = [Cast(f'fin_{t}') for t in PAIR]

    def finish0(t):
        blk = rows(cz * chunk + t * TILE, TILE)
        mark = len(sent)
        ag[t].push(0, [(hb.at[rows(t * TILE, TILE), :], xbuf.at[blk, :])])
        ag_marks.append((mark, len(sent)))
        xbuf[blk, :] = hb[rows(t * TILE, TILE), :]

    pl.run_scoped(lambda wbuf, acc, msend: mlp0(wbuf, acc, msend, h_tx0, ev0, finish0),
                  pltpu.VMEM((2, 4, 3, F_HALF, BLK), BF16), pltpu.VMEM((2 * chunk, 2048), F32), pltpu.VMEM((chunk, 2048), BF16))

    def ag_block(k, t):
        return xbuf.at[rows(slot_plane(k) * chunk + t * TILE, TILE), :]

    def ag_relay(k):
        for t in PAIR:
            ag[t].relay(k, same([ag_block(k, t)]))

    def ag_part(k):
        if k == S2:
            ag_relay(S3)
            for i in TRIO[1:]:
                m1.relay(S1, i)
            m1.got_r0()
            o1.got_xy(S1)
            o1.got_rx0()
            for i in TRIO:
                m1.got_xy(S1, i)
                m1.take(S2, i)
        for t in PAIR:
            ag[t].take(k)
        if k == S3:
            o1.got_xy(S2)
            o1.got_xy(S3)

    def front_one(**kw):
        for t in PAIR:
            for k in (S1, S2):
                ag[t].relay(k, same([ag_block(k, t)]))
        for i in TRIO:
            q1.got_y(i)
        for k in SLOTS:
            o1.take(k)
        o1.got_y0()
        for i in TRIO:
            m1.spread(S1, i)
        for i in TRIO:
            q1.got_r(i)
        q1.done()
        front(1, ag_tx=lambda k: ag_part(k) if k else None, ticks=(tick_d, tick_e, tick_f), mid_hooks=(mid_d, mid_e, mid_f), **kw)

    def tick_d():
        for i in TRIO:
            m1.relay(S3, i)

    def tick_e():
        for i in TRIO:
            m1.got_r(S1, i)

    def mid_d():
        for i in TRIO:
            m1.got_xy(S2, i)

    def mid_e():
        m1.take(S3, 0)

    def mid_f():
        m1.take(S3, TRIO[1])

    def tick_f():
        for k in SLOTS:
            o1.got_r(k)
        o1.done()
        for i in TRIO:
            m1.got_r(S2, i)
        m1.take(S3, TRIO[2])
        m1.got_xy(S3, 0)
        m1.got_xy(S3, TRIO[1])

    pl.run_scoped(front_one, **front_scope)
    for first, last in ag_marks:
        flush(first, last)
    pl.run_scoped(lambda wo: proj(1, wo, None), pltpu.VMEM((4, 4, BLK, BLK), BF16))

    def last_relays():
        m1.got_xy(S3, TRIO[2])
        m1.got_r(S3, 0)

    def last_blocks():
        for i in TRIO[1:]:
            m1.got_r(S3, i)

    ev1 = (last_relays, nothing, nothing, last_blocks)

    def finish1(t):
        blk = rows(cz * chunk + t * TILE, TILE)
        fin[t].push(0, [(hb.at[rows(t * TILE, TILE), :], y_ref.at[blk, :])])
        local(hb.at[rows(t * TILE, TILE), :], y_ref.at[blk, :], 1 + t)

    pl.run_scoped(lambda wbuf, acc: mlp1(wbuf, acc, ev1, finish1),
                  pltpu.VMEM((2, 4, 3, 1376, BLK), BF16), pltpu.VMEM((chunk, 2048), F32))
    def fin_block(k, t):
        return y_ref.at[rows(slot_plane(k) * chunk + t * TILE, TILE), :]

    for k in SLOTS:
        for t in PAIR:
            fin[t].relay(k, same([fin_block(k, t)]))
    for k in SLOTS:
        for t in PAIR:
            fin[t].take(k)
    for t in PAIR:
        pltpu.make_async_copy(hb.at[rows(t * TILE, TILE), :], y_ref.at[rows(t * TILE, TILE), :], loc_sems.at[1 + t]).wait()
    flush()
    assert max(state.values()) <= N_SEM, state


def mega_call(x, wq, wk, wv, wo, wg, wu, wd, gains, tab):
    seq, width = x.shape
    any_spec = pl.BlockSpec(memory_space=pl.ANY)
    chunk = seq // 4
    outs = [jax.ShapeDtypeStruct((seq, width), BF16),
            jax.ShapeDtypeStruct((2, seq, BLK), BF16), jax.ShapeDtypeStruct((2, seq, BLK), BF16),
            jax.ShapeDtypeStruct((2, 3, 2048, BLK), BF16), jax.ShapeDtypeStruct((2, 4, 4, BLK, BLK), BF16),
            jax.ShapeDtypeStruct((4, 4, 3, F_HALF, BLK), BF16), jax.ShapeDtypeStruct((4, 4, 3, 1376, BLK), BF16)]
    return pl.pallas_call(
        mega,
        in_specs=[any_spec] * 10,
        out_specs=[any_spec] * 7,
        out_shape=outs,
        scratch_shapes=[pltpu.VMEM((seq, width), BF16), pltpu.VMEM((2 * chunk, width), BF16)] + [pltpu.VMEM((chunk, width), BF16)] + [
                        pltpu.VMEM((2, chunk, width), BF16), pltpu.VMEM((2, 4, 8, seq), F32),
                        pltpu.VMEM((seq, LANE), F32), pltpu.VMEM((seq, LANE), F32), pltpu.VMEM((4, 8, BLK), F32),
                        pltpu.SemaphoreType.DMA((N_SEM,)), pltpu.SemaphoreType.DMA((N_SEM,)),
                        pltpu.SemaphoreType.DMA((32,))],
        compiler_params=pltpu.CompilerParams(has_side_effects=True, vmem_limit_bytes=67043328),
        name='mega')(x, wq, wk, wv, wo, wg, wu, wd, gains, tab)


def solution(mesh):
    batch_axes = ('dp', 'fsdp')
    act_spec = P(batch_axes, None, None)
    in_cols = P(None, 'fsdp', 'tp')
    in_rows = P(None, 'tp', 'fsdp')
    tp_gain = P(None, 'tp')
    fsdp_gain = P(None, 'fsdp')
    cache_spec = P(None, batch_axes, None, 'tp', None)

    def local_layers(x, w_query, w_key, w_value, w_out, w_gate, w_up, w_down, q_norm_w, k_norm_w, attn_norm_w, ffn_norm_w):
        batch, seq_len, width = x.shape
        gains = jnp.concatenate([attn_norm_w, ffn_norm_w, q_norm_w, k_norm_w], axis=0)
        tab = jnp.asarray(rope_table(seq_len))
        outs = mega_call(x.reshape(seq_len, width), w_query, w_key, w_value, w_out,
                         jnp.swapaxes(w_gate, 1, 2), jnp.swapaxes(w_up, 1, 2), w_down, gains, tab)
        shape = (2, 1, seq_len, 4, HEAD_DIM)
        return outs[0].reshape(x.shape), outs[1].reshape(shape), outs[2].reshape(shape)

    return jax.shard_map(local_layers, mesh=mesh,
                         in_specs=(act_spec, in_cols, in_cols, in_cols, in_rows, in_cols, in_cols, in_rows,
                                   tp_gain, tp_gain, fsdp_gain, fsdp_gain),
                         out_specs=(act_spec, cache_spec, cache_spec), check_vma=False)
```

time: 1940 us -> 779 us (0.40)
  waiting for transfers between devices: 1320 us -> 0 us
  Pallas kernels: 0 us -> 742 us
  matrix products: 337 us -> 0 us
  other arithmetic: 107 us -> 1.36 us
  local copies, waits for them, and re-layouts: 85.4 us -> 22.2 us
  blocking collectives: 58.6 us -> 0 us
    psum x4 -> x0, waiting for transfers between devices: 1080 us -> none  [the longest x2 550 us: local_layers(): a_out = lax.psum(a_part, 'tp').astype(jnp.float32)]
    pallas_call x0 -> x1, Pallas kernels: none -> 742 us  [mega_call(): pl.pallas_call(mega, in_specs=[any_spec] * 10, out_specs=[any_spec] * 7,...]
    dot_general x14 -> x0, matrix products: 269 us -> none  [the longest x2 77.5 us: attend(): jnp.einsum('bhqk,bkhd->bqhd', attn_probs, values, preferred_element_type=...]
    all_gather x14 -> x0, waiting for transfers between devices: 243 us -> none  [the longest x2 88.8 us: local_layers(): wd_full = lax.all_gather(w_down[layer], 'fsdp', axis=1, tiled=True)]
    sub x2 -> x0, matrix products: 67.4 us -> none  [attend(): attn_probs = jax.nn.softmax(scores, axis=-1).astype(jnp.bfloat16)]
    unnamed x53 -> x1, local copies, waits for them, and re-layouts: 53.7 us -> 8.44 us
    psum x2 -> x0, blocking collectives: 38 us -> none  [local_layers(): sq_total = lax.psum(sq_local, 'tp')]
    convert_element_type x3 -> x0, other arithmetic: 28 us -> none  [the longest x2 18.6 us: local_layers(): (hidden.astype(jnp.float32) + a_out * rms_scale(a_out) * attn_gain).astyp...]
  transfers between devices with their start and end apart: 18 -> 0, of which waited for: 14 -> 0; matrix products, arithmetic and copies ran while one was open for 22% -> 0% of each run, Pallas kernels for 0% -> 0%
where the time goes in v2:
time: 779 us; the launch traced here: 766 us
  Pallas kernels  742 us (95%)
  local copies, waits for them, and re-layouts  22.2 us (3%)
    pallas_call x1, Pallas kernels, mega_call(): pl.pallas_call(mega, in_specs=[any_spec] * 10, out_specs=[any_spec] * 7,...  742 us

profile of v2, /device:TPU:0, one launch (start us, length us, event | category | flops | bytes accessed | tf_op | source)
XLA Modules:
  0.0 766.5 jit_solution(2742438144507907837)
XLA Ops:
  0.6 1.4 pad_maximum_fusion.gain_ref
  2.0 741.8 %mega.1 = (bf16[2048,2048]{1,0:T(8,128)(2,1)}, bf16[2,2048,512]{2,1,0:T(8,128)(2,1)}, bf16[2,2048,512]{2,1,0:T(8,128)(2,1)}, bf16[2,3,2048,512]{3,2,1,0:T(8,128)...) custom-call(bf16[2048,2048]{1,0:T(8,128)(2,1)} %bitcast.6, ...), custom_call_target="tpu_custom_call" | custom-call | tf_op jit(solution)/shard_map/mega/pallas_call | solution.py:927
  743.8 6.9 reshape.20
  750.7 6.9 reshape.21
  757.6 8.4 %copy.19 = bf16[1,2048,2048]{2,1,0:T(8,128)(2,1)} copy(bf16[1,2048,2048]{2,1,0:T(8,128)(2,1)} %bitcast.7) | data formatting | bytes 16777216

commit v3 on v2

--- a/solution.py
+++ b/solution.py
@@ -370,12 +370,21 @@
                 self.wait('c0', 'd0')
             else:
                 for i in TRIO:
-                    self.wait(f'c{k}{i}', f'd{k}{i}')
+                    self.done_part(k, i)
+
+        def done_part(self, k, i):
+            self.wait(f'c{k}{i}', f'd{k}{i}')
 
     def local(src, dst, n):
         cp = pltpu.make_async_copy(src, dst, loc_sems.at[n])
         cp.start()
         return cp
+
+    gate_sem = pltpu.get_barrier_semaphore()
+    partners = [X] + [(cx, cz, (cf + off) % 4) for off in SLOTS] + [(cx, (cz + off) % 4, cf) for off in SLOTS]
+    for dev in partners:
+        pl.semaphore_signal(gate_sem, inc=1, device_id=dev, device_id_type=MESH)
+    pl.semaphore_wait(gate_sem, len(partners))
 
     q0, o0, m0 = QGroup('q', 0), OGroup('o', 0), MGroup('m', 0)
     q1, o1, m1 = QGroup('q', 1), OGroup('o', 1), WideGroup('m', 1)
@@ -405,27 +414,29 @@
     with jax.named_scope('tables'):
         loop(seq // TILE, make_tables)
 
-    o0.relay(1)
-    o0.relay(2)
+    o0.relay(S1)
+    o0.relay(S2)
     m0.begin_ring()
-    o0.take(1)
+    o0.take(S1)
     for i in TRIO:
         q0.got_y(i)
-    o0.relay(3)
+    o0.relay(S3)
     o0.got_y0()
     for i in TRIO:
         q0.got_r(i)
     for tx in gain_tx:
         arrive(tx)
     q0.done()
-    m0.relay('a', 1)
-    m0.relay('a', 2)
+    m0.relay('a', S1)
+    m0.relay('a', S2)
     ld_x.wait()
     ld_g.wait()
     ld_h.wait()
 
     def gain_row(i):
         return jnp.concatenate([gp[f, i:i + 1, :] for f in QUAD], axis=1)
+
+    o_recv = [[], []]
 
     def front(layer, wqkv, raw, qkv, obuf, ag_tx, ticks, mid_hooks):
         loads = [local(aq_ref.at[layer, i, rows(((cf + j) % 4) * BLK, BLK), :],
@@ -537,35 +548,40 @@
             j = (cz + o) % 4
             cp = pltpu.make_async_remote_copy(
                 src_ref=obuf.at[rows(j * chunk, chunk), :],
-                dst_ref=ofull.at[layer, :, pl.ds(pl.multiple_of(cz * BLK, BLK), BLK)],
+                dst_ref=ofull.at[:, pl.ds(pl.multiple_of(cz * BLK, BLK), BLK)],
                 send_sem=send_sems.at[m], recv_sem=recv_sems.at[n], device_id=(cx, j, cf), device_id_type=MESH)
             o_tx.append(cp)
+            o_recv[layer].append((n, frozen(ofull.at[:, pl.ds(0, BLK)])))
         with jax.named_scope('attend'):
             loop(4, attend_all)
-        ofull[layer, :, pl.ds(pl.multiple_of(cz * BLK, BLK), BLK)] = obuf[rows(cz * chunk, chunk), :]
+        ofull[:, pl.ds(pl.multiple_of(cz * BLK, BLK), BLK)] = obuf[rows(cz * chunk, chunk), :]
         ticks[2]()
         cp_v.wait()
         cp_k.wait()
-        with jax.named_scope('wait_o'):
-            for cp in o_tx:
-                cp.wait_send()
-                cp.wait_recv()
-
-    def proj(layer, wo, h_tx):
-        loads = []
-        for p in QUAD:
-            for f in QUAD:
-                n = 4 + p * 4 + f
-                mine = jnp.logical_and(cz == p, cf == f)
-
-                @pl.when(mine)
-                def _():
-                    local(wo_ref.at[layer], wo.at[p, f], n)
-
-                @pl.when(jnp.logical_not(mine))
-                def _():
-                    local(ao_ref.at[layer, p, f], wo.at[p, f], n)
-                loads.append(pltpu.make_async_copy(wo_ref.at[layer], wo.at[p, f], loc_sems.at[n]))
+        for cp in o_tx:
+            cp.wait_send()
+
+    def wo_waits(layer, wo_at):
+        return [pltpu.make_async_copy(wo_ref.at[layer], wo_at(n), loc_sems.at[40 + n]) for n in range(16)]
+
+    def wo_loads(layer, wo_at):
+        for n in range(16):
+            p, f = n // 4, n % 4
+            mine = jnp.logical_and(cz == p, cf == f)
+
+            @pl.when(mine)
+            def _():
+                local(wo_ref.at[layer], wo_at(n), 40 + n)
+
+            @pl.when(jnp.logical_not(mine))
+            def _():
+                local(ao_ref.at[layer, p, f], wo_at(n), 40 + n)
+
+    def wo_in_x(n):
+        return xbuf.at[rows(n // 4 * BLK, BLK), pl.ds(n % 4 * BLK, BLK)]
+
+    def proj(layer, wo_at, loads, h_tx):
+        arrive(o_recv[layer], 'wait_o')
         with jax.named_scope('wait_wo'):
             for cp in loads:
                 cp.wait()
@@ -573,12 +589,12 @@
 
         def tile(t):
             r = rows(t * TILE, TILE)
-            ot = ofull[layer, r, :]
+            ot = ofull[r, :]
             parts = []
             for f in QUAD:
-                acc = dot_nn(ot[:, 0:BLK], wo[0, f])
+                acc = dot_nn(ot[:, 0:BLK], wo_at(f)[...])
                 for p in SLOTS:
-                    acc = acc + dot_nn(ot[:, p * BLK:(p + 1) * BLK], wo[p, f])
+                    acc = acc + dot_nn(ot[:, p * BLK:(p + 1) * BLK], wo_at(p * 4 + f)[...])
                 parts.append(acc.astype(BF16).astype(F32))
             a = jnp.concatenate(parts, axis=1)
             scale = lax.rsqrt(jnp.mean(a * a, axis=-1, keepdims=True) + NORM_EPS)
@@ -591,24 +607,29 @@
                 mark = len(sent)
                 h_tx.append((mark, remote([(hb.at[rows(t * TILE, TILE), :], hb.at[rows(chunk + t * TILE, TILE), :])], Y)))
 
-    def mlp_tile(k, t, w, acc, out=None):
-        r = rows(t * TILE, TILE)
-        ht = hb[r, :]
+    def mlp_act(t, w):
+        ht = hb[rows(t * TILE, TILE), :]
         gate = dot_nt(ht[:, 0:BLK], w[0, 0])
         up = dot_nt(ht[:, 0:BLK], w[0, 1])
-        for f in SLOTS:
+        for f in range(1, 4):
             gate = gate + dot_nt(ht[:, f * BLK:(f + 1) * BLK], w[f, 0])
             up = up + dot_nt(ht[:, f * BLK:(f + 1) * BLK], w[f, 1])
-        act = (jax.nn.silu(gate) * up).astype(BF16)
+        return (jax.nn.silu(gate) * up).astype(BF16)
+
+    def mlp_down(first, t, act, w, acc, out=None):
+        r = rows(t * TILE, TILE)
         for f in QUAD:
             c = slice(f * BLK, (f + 1) * BLK)
             val = dot_nn(act, w[f, 2])
-            if k:
+            if not first:
                 val = val + acc[r, c]
             if out is None:
                 acc[r, c] = val
             else:
                 out[rows(t * TILE - chunk, TILE), c] = val.astype(BF16)
+
+    def mlp_tile(first, t, w, acc, out=None):
+        mlp_down(first, t, mlp_act(t, w), w, acc, out)
 
     def fetch0(k, wbuf):
         s = k % 2
@@ -623,8 +644,7 @@
                 cps.append(local(aw_ref.at[p, f], wbuf.at[s, f], 4 + s * 6 + (j - 1 if j else 3)))
         return cps
 
-    def fetch1(k, wbuf):
-        s = k % 2
+    def fetch1(k, s, wbuf):
         p = m1.plane(k)
         cps = []
         for j in QUAD:
@@ -653,30 +673,30 @@
         m0.done(0)
         settle(fetch0(0, wbuf))
         with jax.named_scope('mlp0_own'):
-            loop(2, lambda t: mlp_tile(0, t, wbuf.at[0], acc))
+            loop(2, lambda t: mlp_tile(True, t, wbuf.at[0], acc))
         ev[7]()
         for _, tx in h_tx:
             arrive(tx, 'wait_h')
         with jax.named_scope('mlp0_other'):
-            loop(2, lambda t: mlp_tile(0, t + 2, wbuf.at[0], acc))
+            loop(2, lambda t: mlp_tile(True, t + 2, wbuf.at[0], acc))
         for k in (1, 2):
             ev[k]()
             m0.done(k)
             settle(fetch0(k, wbuf))
             with jax.named_scope('mlp0'):
-                loop(4, lambda t: mlp_tile(k, t, wbuf.at[k % 2], acc))
+                loop(4, lambda t: mlp_tile(False, t, wbuf.at[k % 2], acc))
         ev[3]()
         m0.done(3)
         settle(fetch0(3, wbuf))
         m_tx = []
         for t in PAIR:
             with jax.named_scope('mlp0_last'):
-                mlp_tile(3, t + 2, wbuf.at[1], acc, msend)
+                mlp_tile(False, t + 2, wbuf.at[1], acc, msend)
             r = rows(t * TILE, TILE)
             mark = len(sent)
             m_tx.append((mark, remote([(msend.at[r, :], mrecv.at[r, :])], Y)))
         with jax.named_scope('mlp0_own'):
-            loop(2, lambda t: mlp_tile(3, t, wbuf.at[1], acc))
+            loop(2, lambda t: mlp_tile(False, t, wbuf.at[1], acc))
         ev[4]()
         for mark, _ in h_tx:
             flush(mark, mark + 1)
@@ -688,28 +708,51 @@
         for mark, _ in m_tx:
             flush(mark, mark + 1)
 
-    def mlp1(wbuf, acc, ev, finish):
-        ev[0]()
+    def mlp1(wbuf, acc, finish):
+        spare = (rows(chunk, TILE), pl.ds(0, 2 * F_HALF))
+
+        def run(k, slot, t, first=False):
+            with jax.named_scope(f'mlp1_{t}_{k}'):
+                mlp_tile(first, t, wbuf.at[slot], acc)
+
         m1.done(0)
-        cps = fetch1(0, wbuf)
-        for k in QUAD:
-            settle(cps)
-            if k < 2:
-                ev[k + 1]()
-                m1.done(k + 1)
-                cps = fetch1(k + 1, wbuf)
-            if k < 3:
-                with jax.named_scope('mlp1'):
-                    loop(2, lambda t: mlp_tile(k, t, wbuf.at[k % 2], acc))
-                if k == 2:
-                    ev[3]()
-                    m1.done(3)
-                    cps = fetch1(3, wbuf)
-            else:
-                for t in PAIR:
-                    with jax.named_scope('mlp1_last'):
-                        mlp_tile(3, t, wbuf.at[1], acc)
-                    close(1, t, acc[rows(t * TILE, TILE), :], finish)
+        cps = fetch1(0, 0, wbuf)
+        proj(1, wo_in_x, wo_waits(1, wo_in_x), None)
+        m1.take(S3, S2)
+        m1.done(S1)
+        settle(cps)
+        cps = fetch1(S1, 1, wbuf)
+        run(0, 0, 0, True)
+        settle(cps)
+        m1.done(S2)
+        cps = fetch1(S2, 0, wbuf)
+        run(S1, 1, 0)
+        for i in PAIR:
+            m1.got_r(S3, i)
+        settle(cps)
+        run(S2, 0, 0)
+        m1.got_xy(S3, S2)
+        p = m1.plane(S3)
+        for i in PAIR:
+            m1.done_part(S3, i)
+        settle([local(bw_ref.at[p, f, pl.ds(0, 2)], wbuf.at[1, f, pl.ds(0, 2)], 4 + f) for f in QUAD])
+        with jax.named_scope('mlp1_act'):
+            hb[spare] = mlp_act(0, wbuf.at[1])
+        m1.got_r(S3, S2)
+        m1.done_part(S3, S2)
+        settle([local(bw_ref.at[p, f, S2], wbuf.at[1, f, S2], 4 + f) for f in QUAD])
+        with jax.named_scope('mlp1_down'):
+            mlp_down(False, 0, hb[spare], wbuf.at[1], acc)
+        close(1, 0, acc[rows(0, TILE), :], finish)
+        run(S2, 0, 1, True)
+        cps = fetch1(0, 0, wbuf)
+        run(S3, 1, 1)
+        settle(cps)
+        cps = fetch1(S1, 1, wbuf)
+        run(0, 0, 1)
+        settle(cps)
+        run(S1, 1, 1)
+        close(1, 1, acc[rows(TILE, TILE), :], finish)
 
     front_scope = dict(wqkv=pltpu.VMEM((3, seq, BLK), BF16), raw=pltpu.VMEM((2, seq, BLK), F32),
                        qkv=pltpu.VMEM((3, seq, BLK), BF16), obuf=pltpu.VMEM((seq, BLK), BF16))
@@ -727,12 +770,11 @@
         o0.got_rx0()
 
     def mid_a():
-        o0.got_xy(S1)
-        o0.got_xy(S2)
+        for k in SLOTS:
+            o0.got_xy(k)
+
+    def mid_b():
         m0.take('a', S2)
-
-    def mid_b():
-        o0.got_xy(S3)
 
     def mid_c():
         m0.got_x('a', S1)
@@ -741,6 +783,7 @@
 
     def tick_c():
         m0.begin_y_rest()
+        q1.begin()
         for k in SLOTS:
             o0.got_r(k)
         o0.done()
@@ -748,11 +791,22 @@
 
     pl.run_scoped(lambda **kw: front(0, ag_tx=None, ticks=(tick_a, tick_b, tick_c), mid_hooks=(mid_a, mid_b, mid_c), **kw), **front_scope)
     h_tx0 = []
-    pl.run_scoped(lambda wo: proj(0, wo, h_tx0), pltpu.VMEM((4, 4, BLK, BLK), BF16))
+
+    def proj_zero(wo):
+        def wo_at(n):
+            return wo.at[n]
+
+        wo_loads(0, wo_at)
+        proj(0, wo_at, wo_waits(0, wo_at), h_tx0)
+
+    pl.run_scoped(proj_zero, pltpu.VMEM((16, BLK, BLK), BF16))
 
     def before_own():
         m0.relay('b', S3)
         m0.take('a', S3)
+        o1.begin()
+        for i in TRIO:
+            m1.begin_ring(i)
         m0.got_yb()
         m0.got_x('a', S2)
         m0.got_x('b', S1)
@@ -762,40 +816,36 @@
     def before_other():
         m0.take('b', S2)
         m0.take('b', S3)
-        o1.begin()
+        m0.got_x('a', S3)
         for i in TRIO:
-            m1.begin_ring(i)
-        m0.got_x('a', S3)
-
-    def before_one():
+            q1.got_y(i)
         o1.relay(S1)
         o1.relay(S2)
 
-    def before_two():
+    def before_one():
         m0.got_x('b', S2)
-        o1.relay(S3)
-
-    def before_three():
-        m0.got_x('b', S3)
         m1.relay(S1, 0)
         m1.relay(S2, 0)
 
-    def before_sum():
-        for i in TRIO:
-            m1.got_y0(i)
+    def before_two():
+        m0.got_x('b', S3)
         m1.take(S1, 0, spread=False)
         for i in TRIO[1:]:
             m1.relay(S2, i)
 
-    def after_first():
-        m1.take(S1, TRIO[1], spread=False)
+    def before_three():
+        o1.relay(S3)
+        m1.got_y0(0)
+
+    def before_sum():
+        for i in TRIO[1:]:
+            m1.got_y0(i)
+            m1.take(S1, i, spread=False)
 
     def after_second():
-        q1.begin()
         o1.begin_y()
-        m1.take(S1, TRIO[2], spread=False)
-
-    ev0 = (before_own, before_one, before_two, before_three, before_sum, after_first, after_second, before_other)
+
+    ev0 = (before_own, before_one, before_two, before_three, before_sum, nothing, after_second, before_other)
 
     ag_marks = []
     ag = [Cast(f'ag_{t}') for t in PAIR]
@@ -814,9 +864,14 @@
     def ag_block(k, t):
         return xbuf.at[rows(slot_plane(k) * chunk + t * TILE, TILE), :]
 
+    def ag_pass(t, k):
+        mark = len(sent)
+        ag[t].relay(k, same([ag_block(k, t)]))
+        ag_marks.append((mark, len(sent)))
+
     def ag_relay(k):
         for t in PAIR:
-            ag[t].relay(k, same([ag_block(k, t)]))
+            ag_pass(t, k)
 
     def ag_part(k):
         if k == S2:
@@ -828,78 +883,65 @@
             o1.got_rx0()
             for i in TRIO:
                 m1.got_xy(S1, i)
-                m1.take(S2, i)
         for t in PAIR:
             ag[t].take(k)
-        if k == S3:
-            o1.got_xy(S2)
-            o1.got_xy(S3)
+            if k == S3 and t == 0:
+                o1.got_xy(S2)
+                o1.got_xy(S3)
+                for i in TRIO:
+                    m1.got_xy(S2, i)
 
     def front_one(**kw):
         for t in PAIR:
             for k in (S1, S2):
-                ag[t].relay(k, same([ag_block(k, t)]))
+                ag_pass(t, k)
         for i in TRIO:
-            q1.got_y(i)
+            m1.spread(S1, i)
         for k in SLOTS:
             o1.take(k)
+        for i in TRIO:
+            m1.take(S2, i)
         o1.got_y0()
-        for i in TRIO:
-            m1.spread(S1, i)
         for i in TRIO:
             q1.got_r(i)
         q1.done()
-        front(1, ag_tx=lambda k: ag_part(k) if k else None, ticks=(tick_d, tick_e, tick_f), mid_hooks=(mid_d, mid_e, mid_f), **kw)
+        front(1, ag_tx=lambda k: ag_part(k) if k else None, ticks=(tick_d, tick_e, tick_f), mid_hooks=(nothing, mid_e, nothing), **kw)
 
     def tick_d():
-        for i in TRIO:
+        for i in PAIR:
             m1.relay(S3, i)
 
     def tick_e():
         for i in TRIO:
             m1.got_r(S1, i)
-
-    def mid_d():
-        for i in TRIO:
-            m1.got_xy(S2, i)
-
-    def mid_e():
-        m1.take(S3, 0)
-
-    def mid_f():
-        m1.take(S3, TRIO[1])
-
-    def tick_f():
         for k in SLOTS:
             o1.got_r(k)
         o1.done()
+        for first, last in ag_marks:
+            flush(first, last)
+        wo_loads(1, wo_in_x)
+
+    def mid_e():
+        m1.take(S3, 0)
+
+    def tick_f():
+        m1.relay(S3, S2)
         for i in TRIO:
             m1.got_r(S2, i)
-        m1.take(S3, TRIO[2])
-        m1.got_xy(S3, 0)
-        m1.got_xy(S3, TRIO[1])
+        m1.take(S3, S1)
+        for i in PAIR:
+            m1.got_xy(S3, i)
 
     pl.run_scoped(front_one, **front_scope)
     for first, last in ag_marks:
         flush(first, last)
-    pl.run_scoped(lambda wo: proj(1, wo, None), pltpu.VMEM((4, 4, BLK, BLK), BF16))
-
-    def last_relays():
-        m1.got_xy(S3, TRIO[2])
-        m1.got_r(S3, 0)
-
-    def last_blocks():
-        for i in TRIO[1:]:
-            m1.got_r(S3, i)
-
-    ev1 = (last_relays, nothing, nothing, last_blocks)
 
     def finish1(t):
         blk = rows(cz * chunk + t * TILE, TILE)
         fin[t].push(0, [(hb.at[rows(t * TILE, TILE), :], y_ref.at[blk, :])])
         local(hb.at[rows(t * TILE, TILE), :], y_ref.at[blk, :], 1 + t)
 
-    pl.run_scoped(lambda wbuf, acc: mlp1(wbuf, acc, ev1, finish1),
+    pl.run_scoped(lambda wbuf, acc: mlp1(wbuf, acc, finish1),
                   pltpu.VMEM((2, 4, 3, 1376, BLK), BF16), pltpu.VMEM((chunk, 2048), F32))
     def fin_block(k, t):
         return y_ref.at[rows(slot_plane(k) * chunk + t * TILE, TILE), :]
@@ -907,6 +949,7 @@
     for k in SLOTS:
         for t in PAIR:
             fin[t].relay(k, same([fin_block(k, t)]))
+    flush()
     for k in SLOTS:
         for t in PAIR:
             fin[t].take(k)
@@ -930,11 +973,11 @@
         out_specs=[any_spec] * 7,
         out_shape=outs,
         scratch_shapes=[pltpu.VMEM((seq, width), BF16), pltpu.VMEM((2 * chunk, width), BF16)] + [pltpu.VMEM((chunk, width), BF16)] + [
-                        pltpu.VMEM((2, chunk, width), BF16), pltpu.VMEM((2, 4, 8, seq), F32),
+                        pltpu.VMEM((chunk, width), BF16), pltpu.VMEM((2, 4, 8, seq), F32),
                         pltpu.VMEM((seq, LANE), F32), pltpu.VMEM((seq, LANE), F32), pltpu.VMEM((4, 8, BLK), F32),
                         pltpu.SemaphoreType.DMA((N_SEM,)), pltpu.SemaphoreType.DMA((N_SEM,)),
-                        pltpu.SemaphoreType.DMA((32,))],
-        compiler_params=pltpu.CompilerParams(has_side_effects=True, vmem_limit_bytes=67043328),
+                        pltpu.SemaphoreType.DMA((64,))],
+        compiler_params=pltpu.CompilerParams(collective_id=0, has_side_effects=True, vmem_limit_bytes=67043328),
         name='mega')(x, wq, wk, wv, wo, wg, wu, wd, gains, tab)
 
 

time: 779 us -> 743 us (0.954)
  Pallas kernels: 742 us -> 709 us
    pallas_call x1, Pallas kernels: 742 us -> 709 us  [mega_call(): pl.pallas_call(mega, in_specs=[any_spec] * 10, out_specs=[any_spec] * 7,...]
where the time goes in v3:
time: 743 us; the launch traced here: 734 us
  Pallas kernels  709 us (95%)
  local copies, waits for them, and re-layouts  22.2 us (3%)
    pallas_call x1, Pallas kernels, mega_call(): pl.pallas_call(mega, in_specs=[any_spec] * 10, out_specs=[any_spec] * 7,...  709 us

profile of v3, /device:TPU:0, one launch (start us, length us, event | category | flops | bytes accessed | tf_op | source)
XLA Modules:
  0.0 733.7 jit_solution(7824915273306974390)
XLA Ops:
  0.6 1.4 pad_maximum_fusion.gain_ref
  2.0 709.1 %mega.1 = (bf16[2048,2048]{1,0:T(8,128)(2,1)}, bf16[2,2048,512]{2,1,0:T(8,128)(2,1)}, bf16[2,2048,512]{2,1,0:T(8,128)(2,1)}, bf16[2,3,2048,512]{3,2,1,0:T(8,128)...) custom-call(bf16[2048,2048]{1,0:T(8,128)(2,1)} %bitcast.6, ...), custom_call_target="tpu_custom_call" | custom-call | tf_op jit(solution)/shard_map/mega/pallas_call | solution.py:970
  711.1 6.9 reshape.20
  718.0 6.9 reshape.21
  724.9 8.4 %copy.19 = bf16[1,2048,2048]{2,1,0:T(8,128)(2,1)} copy(bf16[1,2048,2048]{2,1,0:T(8,128)(2,1)} %bitcast.7) | data formatting | bytes 16777216
